TPU v7x, 8 devices: a whole 2x2x1 slice. The times are simulated.
8 devices in a mesh: parts: 1 (over z), tiley: 2 (over y), tilex: 4 (over x, core).
Axes of the slice: x: 2, y: 2, z: 1, core: 2. Of those that a mesh axis runs over, the one named last changes fastest.
Arguments:
- node_feats: bfloat16 [16384, 1433], P(('parts', 'tiley', 'tilex'))
- adj_int: bfloat16 [16384, 2048], P(('parts', 'tiley', 'tilex'))
- adj_halo: bfloat16 [16384, 1024], P(('parts', 'tiley', 'tilex'))
- send_idx: int32 [32, 256], P(('parts', 'tiley', 'tilex'))
- w_hidden: bfloat16 [1433, 16], replicated
- w_out: bfloat16 [16, 7], replicated
Outputs:
- output: bfloat16 [16384, 7], P(('parts', 'tiley', 'tilex'))
All inputs are finite; a program needn't handle non-finite values.
Results may differ from a plain program's by a relative error of at most 0.001.
Values are sent between devices in bfloat16 or wider.
A program may use at most 1 GiB of HBM per device.

v0:
```python
import jax
import jax.numpy as jnp
from jax import lax
from jax.sharding import PartitionSpec as P


def shift_pairs(axis_size, shift_by):
    return [(source, (source + shift_by) % axis_size) for source in range(axis_size)]


def solution(mesh):
    grid_y = mesh.shape['tiley']
    grid_x = mesh.shape['tilex']
    node_spec = P(('parts', 'tiley', 'tilex'), None)
    full_spec = P(None, None)

    def gcn_layer(layer_in, adj_int, adj_halo, send_idx, weight, apply_relu):
        sent_rows = jnp.take(layer_in, send_idx, axis=0)
        from_west = lax.ppermute(sent_rows[0], 'tilex', shift_pairs(grid_x, 1))
        from_east = lax.ppermute(sent_rows[1], 'tilex', shift_pairs(grid_x, -1))
        from_south = lax.ppermute(sent_rows[2], 'tiley', shift_pairs(grid_y, 1))
        from_north = lax.ppermute(sent_rows[3], 'tiley', shift_pairs(grid_y, -1))
        recv_rows = jnp.concatenate([from_west, from_east, from_south, from_north], axis=0)
        agg_sum = jnp.dot(adj_int, layer_in, preferred_element_type=jnp.float32) + jnp.dot(adj_halo, recv_rows, preferred_element_type=jnp.float32)
        mixed_out = jnp.dot(agg_sum.astype(jnp.bfloat16), weight, preferred_element_type=jnp.float32)
        if apply_relu:
            mixed_out = jax.nn.relu(mixed_out)
        return mixed_out.astype(jnp.bfloat16)

    def per_device(node_feats, adj_int, adj_halo, send_idx, w_hidden, w_out):
        hidden = gcn_layer(node_feats, adj_int, adj_halo, send_idx, w_hidden, True)
        return gcn_layer(hidden, adj_int, adj_halo, send_idx, w_out, False)

    return jax.shard_map(per_device, mesh=mesh, in_specs=(node_spec, node_spec, node_spec, node_spec, full_spec, full_spec), out_specs=node_spec, check_vma=False)
```

profile of v0, /device:TPU:0, one launch (start us, length us, event | category | flops | bytes accessed | tf_op | source)
XLA Modules:
  0.0 92.5 jit_solution(13677677027387673028)
XLA Ops:
  0.0 0.0 copy-start
  0.0 0.7 compare_and_fusion
  0.7 0.7 fusion.37
  1.4 8.6 %copy.9 = bf16[2048,1433]{1,0:T(8,128)(2,1)} copy(bf16[2048,1433]{0,1:T(8,128)(2,1)} %param.6) | data formatting | bytes 11739136 | tf_op args[0]
  10.0 10.3 %gather_fusion = bf16[1024,1433]{1,0:T(8,128)(2,1)S(1)} fusion(bf16[2048,1433]{1,0:T(8,128)(2,1)} %copy.9, s32[1024]{0:T(1024)S(1)} %broadcast_clamp_fusion), kind=kCustom, calls=%fused_computation | custom fusion | bytes 5873664 | tf_op jit(solution)/shard_map/jit(_take)/gather | solution.py:18
  20.2 2.8 %copy.10 = bf16[4,256,1433]{1,2,0:T(8,128)(2,1)} copy(bf16[4,256,1433]{2,1,0:T(8,128)(2,1)S(1)} %bitcast.39) | data formatting | bytes 5869568 | tf_op jit(solution)/shard_map/jit(_take)/gather | solution.py:18
  23.0 2.1 %broadcast_select_fusion = bf16[4,256,1433]{1,2,0:T(8,128)(2,1)S(1)} fusion(bf16[4,256,1433]{1,2,0:T(8,128)(2,1)} %copy.10, pred[4,256]{1,0:T(4,128)(4,1)S(1)} %compare_and_fusion), kind=kLoop, calls=%fused_computation.12 | loop fusion | flops 1467392 | bytes 5870592 | tf_op jit(solution)/shard_map/jit(_take)/select_n | solution.py:18
  25.1 0.2 slice_bitcast_fusion.3
  25.3 0.9 collective-permute-start
  26.2 2.5 %collective-permute-start.3 = (bf16[256,1433]{0,1:T(8,128)(2,1)S(1)}, bf16[256,1433]{0,1:T(8,128)(2,1)S(1)}, u32[]{:S(2)}, u32[]{:S(2)}) collective-permute-start(bf16[256,1433]{0,1:T(8,128)(2,1)S(1)} %get-tuple-element.6), channel_id=1, source_target_pairs={{0,4},{4,0},{1,5},{5,1},{2,6},{6,2},{3,7},{7,3}} | collective-permute-start | bytes 2201096 | tf_op jit(solution)/shard_map/ppermute | solution.py:22
  28.7 0.0 collective-permute-start.2
  28.8 1.4 %collective-permute-start.1 = (bf16[256,1433]{0,1:T(8,128)(2,1)S(1)}, bf16[256,1433]{0,1:T(8,128)(2,1)S(1)}, u32[]{:S(2)}, u32[]{:S(2)}) collective-permute-start(bf16[256,1433]{0,1:T(8,128)(2,1)S(1)} %get-tuple-element.8), channel_id=1, source_target_pairs={{0,3},{1,0},{2,1},{3,2},{4,7},{5,4},{6,5},{7,6}} | collective-permute-start | bytes 2201096 | tf_op jit(solution)/shard_map/ppermute | solution.py:20
  30.2 19.2 %fusion.42 = f32[2048,1433]{1,0:T(8,128)} fusion(bf16[2048,2048]{1,0:T(8,128)(2,1)} %param.7, bf16[2048,1433]{0,1:T(8,128)(2,1)} %param.6), kind=kOutput, calls=%fused_computation.40 | convolution fusion | flops 12020875264 | bytes 25997312 | tf_op jit(solution)/shard_map/dot_general | solution.py:24
  49.4 0.0 collective-permute-done
  49.4 0.0 collective-permute-done.3
  49.4 11.4 %collective-permute-done.2 = bf16[256,1433]{0,1:T(8,128)(2,1)S(1)} collective-permute-done((bf16[256,1433]{0,1:T(8,128)(2,1)S(1)}, bf16[256,1433]{0,1:T(8,128)(2,1)S(1)}, u32[]{:S(2)}, u32[]{:S(2)}) %collective-permute-start.2) | collective-permute-done | bytes 733728 | tf_op jit(solution)/shard_map/ppermute | solution.py:21
  60.8 0.0 collective-permute-done.1
  60.8 0.0 copy-done
  60.8 14.2 %fusion.20 = bf16[2048,16]{0,1:T(8,128)(2,1)S(1)} fusion(bf16[1433,16]{0,1:T(8,128)(2,1)S(1)} %copy-done, f32[2048,1433]{1,0:T(8,128)} %fusion.42, bf16[2048,1024]{1,0:T(8,128)(2,1)} %param.8, bf16[256,1433]{0,1:T(8,128)(2,1)S(1)} %collective-permute-done.3, bf16[256,1433]{0,1:T(8,128)(2,1)S(1)} %collective-permute-done.2, ...), kind=kOutput, calls=%fused_computation.16 | convolution fusion | flops 6122024960 | bytes 18979616 | tf_op jit(solution)/shard_map/dot_general | solution.py:25
  75.0 0.3 copy.11
  75.3 3.2 %gather_fusion.1 = bf16[1024,16]{1,0:T(8,128)(2,1)S(1)} fusion(bf16[2048,16]{1,0:T(8,128)(2,1)S(1)} %copy.11, s32[1024]{0:T(1024)S(1)} %broadcast_clamp_fusion), kind=kCustom, calls=%fused_computation.1 | custom fusion | bytes 69632 | tf_op jit(solution)/shard_map/jit(_take)/gather | solution.py:18
  78.5 0.1 copy.12
  78.6 0.9 %collective-permute-start.4 = (bf16[256,16]{0,1:T(8,128)(2,1)S(1)}, bf16[256,16]{0,1:T(8,128)(2,1)S(1)}, u32[]{:S(2)}, u32[]{:S(2)}) collective-permute-start(bf16[256,16]{0,1:T(8,128)(2,1)S(1)} %get-tuple-element.9), channel_id=1, source_target_pairs={{0,1},{1,2},{2,3},{3,0},{4,5},{5,6},{6,7},{7,4}} | collective-permute-start | bytes 24584 | tf_op jit(solution)/shard_map/ppermute | solution.py:19
  79.5 2.0 %collective-permute-start.7 = (bf16[256,16]{0,1:T(8,128)(2,1)S(1)}, bf16[256,16]{0,1:T(8,128)(2,1)S(1)}, u32[]{:S(2)}, u32[]{:S(2)}) collective-permute-start(bf16[256,16]{0,1:T(8,128)(2,1)S(1)} %get-tuple-element.10), channel_id=1, source_target_pairs={{0,4},{4,0},{1,5},{5,1},{2,6},{6,2},{3,7},{7,3}} | collective-permute-start | bytes 24584 | tf_op jit(solution)/shard_map/ppermute | solution.py:22
  81.6 0.0 collective-permute-start.6
  81.6 1.0 %collective-permute-start.5 = (bf16[256,16]{0,1:T(8,128)(2,1)S(1)}, bf16[256,16]{0,1:T(8,128)(2,1)S(1)}, u32[]{:S(2)}, u32[]{:S(2)}) collective-permute-start(bf16[256,16]{0,1:T(8,128)(2,1)S(1)} %get-tuple-element.12), channel_id=1, source_target_pairs={{0,3},{1,0},{2,1},{3,2},{4,7},{5,4},{6,5},{7,6}} | collective-permute-start | bytes 24584 | tf_op jit(solution)/shard_map/ppermute | solution.py:20
  82.6 5.6 %fusion.43 = f32[16,2048]{1,0:T(8,128)S(1)} fusion(bf16[2048,16]{0,1:T(8,128)(2,1)S(1)} %fusion.20, bf16[2048,2048]{1,0:T(8,128)(2,1)} %param.7), kind=kOutput, calls=%fused_computation.41 | convolution fusion | flops 134217728 | bytes 8585216 | tf_op jit(solution)/shard_map/dot_general | solution.py:24
  88.3 0.0 collective-permute-done.4
  88.3 0.0 collective-permute-done.7
  88.3 0.0 collective-permute-done.6
  88.3 0.0 collective-permute-done.5
  88.3 4.1 %convolution_convert_fusion = bf16[2048,7]{0,1:T(8,128)(2,1)} fusion(bf16[16,7]{0,1:T(8,128)(2,1)S(1)} %copy-done.1, f32[16,2048]{1,0:T(8,128)S(1)} %fusion.43, bf16[2048,1024]{1,0:T(8,128)(2,1)} %param.8, bf16[256,16]{0,1:T(8,128)(2,1)S(1)} %collective-permute-done.7, bf16[256,16]{0,1:T(8,128)(2,1)S(1)} %collective-permute-done.6, ...), kind=kOutput, calls=%fused_computation.17 | convolution fusion | flops 67778560 | bytes 4387040 | tf_op jit(solution)/shard_map/dot_general | solution.py:25
  (6 shorter events, 0.0 us)
Async XLA Ops:
  0.0 60.8 %copy-start = (bf16[1433,16]{0,1:T(8,128)(2,1)S(1)}, bf16[1433,16]{0,1:T(8,128)(2,1)}, u32[]{:S(2)}) copy-start(bf16[1433,16]{0,1:T(8,128)(2,1)} %param.10) | copy-start | bytes 137572
  25.3 24.1 %collective-permute-start = (bf16[256,1433]{0,1:T(8,128)(2,1)S(1)}, bf16[256,1433]{0,1:T(8,128)(2,1)S(1)}, u32[]{:S(2)}, u32[]{:S(2)}) collective-permute-start(bf16[256,1433]{0,1:T(8,128)(2,1)S(1)} %get-tuple-element.5), channel_id=1, source_target_pairs={{0,1},{1,2},{2,3},{3,0},{4,5},{5,6},{6,7},{7,4}} | collective-permute-start | bytes 2201096 | tf_op jit(solution)/shard_map/ppermute | solution.py:19
  26.2 23.2 %collective-permute-start.3 = (bf16[256,1433]{0,1:T(8,128)(2,1)S(1)}, bf16[256,1433]{0,1:T(8,128)(2,1)S(1)}, u32[]{:S(2)}, u32[]{:S(2)}) collective-permute-start(bf16[256,1433]{0,1:T(8,128)(2,1)S(1)} %get-tuple-element.6), channel_id=1, source_target_pairs={{0,4},{4,0},{1,5},{5,1},{2,6},{6,2},{3,7},{7,3}} | collective-permute-start | bytes 2201096 | tf_op jit(solution)/shard_map/ppermute | solution.py:22
  28.7 32.1 %collective-permute-start.2 = (bf16[256,1433]{0,1:T(8,128)(2,1)S(1)}, bf16[256,1433]{0,1:T(8,128)(2,1)S(1)}, u32[]{:S(2)}, u32[]{:S(2)}) collective-permute-start(bf16[256,1433]{0,1:T(8,128)(2,1)S(1)} %get-tuple-element.7), channel_id=1, source_target_pairs={{0,4},{4,0},{1,5},{5,1},{2,6},{6,2},{3,7},{7,3}} | collective-permute-start | bytes 2201096 | tf_op jit(solution)/shard_map/ppermute | solution.py:21
  28.8 32.0 %collective-permute-start.1 = (bf16[256,1433]{0,1:T(8,128)(2,1)S(1)}, bf16[256,1433]{0,1:T(8,128)(2,1)S(1)}, u32[]{:S(2)}, u32[]{:S(2)}) collective-permute-start(bf16[256,1433]{0,1:T(8,128)(2,1)S(1)} %get-tuple-element.8), channel_id=1, source_target_pairs={{0,3},{1,0},{2,1},{3,2},{4,7},{5,4},{6,5},{7,6}} | collective-permute-start | bytes 2201096 | tf_op jit(solution)/shard_map/ppermute | solution.py:20
  75.0 13.4 %copy-start.1 = (bf16[16,7]{0,1:T(8,128)(2,1)S(1)}, bf16[16,7]{0,1:T(8,128)(2,1)}, u32[]{:S(2)}) copy-start(bf16[16,7]{0,1:T(8,128)(2,1)} %param.11) | copy-start | bytes 676
  78.6 9.7 %collective-permute-start.4 = (bf16[256,16]{0,1:T(8,128)(2,1)S(1)}, bf16[256,16]{0,1:T(8,128)(2,1)S(1)}, u32[]{:S(2)}, u32[]{:S(2)}) collective-permute-start(bf16[256,16]{0,1:T(8,128)(2,1)S(1)} %get-tuple-element.9), channel_id=1, source_target_pairs={{0,1},{1,2},{2,3},{3,0},{4,5},{5,6},{6,7},{7,4}} | collective-permute-start | bytes 24584 | tf_op jit(solution)/shard_map/ppermute | solution.py:19
  79.5 8.7 %collective-permute-start.7 = (bf16[256,16]{0,1:T(8,128)(2,1)S(1)}, bf16[256,16]{0,1:T(8,128)(2,1)S(1)}, u32[]{:S(2)}, u32[]{:S(2)}) collective-permute-start(bf16[256,16]{0,1:T(8,128)(2,1)S(1)} %get-tuple-element.10), channel_id=1, source_target_pairs={{0,4},{4,0},{1,5},{5,1},{2,6},{6,2},{3,7},{7,3}} | collective-permute-start | bytes 24584 | tf_op jit(solution)/shard_map/ppermute | solution.py:22
  81.6 6.7 %collective-permute-start.6 = (bf16[256,16]{0,1:T(8,128)(2,1)S(1)}, bf16[256,16]{0,1:T(8,128)(2,1)S(1)}, u32[]{:S(2)}, u32[]{:S(2)}) collective-permute-start(bf16[256,16]{0,1:T(8,128)(2,1)S(1)} %get-tuple-element.11), channel_id=1, source_target_pairs={{0,4},{4,0},{1,5},{5,1},{2,6},{6,2},{3,7},{7,3}} | collective-permute-start | bytes 24584 | tf_op jit(solution)/shard_map/ppermute | solution.py:21
  81.6 6.7 %collective-permute-start.5 = (bf16[256,16]{0,1:T(8,128)(2,1)S(1)}, bf16[256,16]{0,1:T(8,128)(2,1)S(1)}, u32[]{:S(2)}, u32[]{:S(2)}) collective-permute-start(bf16[256,16]{0,1:T(8,128)(2,1)S(1)} %get-tuple-element.12), channel_id=1, source_target_pairs={{0,3},{1,0},{2,1},{3,2},{4,7},{5,4},{6,5},{7,6}} | collective-permute-start | bytes 24584 | tf_op jit(solution)/shard_map/ppermute | solution.py:20
where the time goes:
time: 92.9 us; the launch traced here: 92.5 us
  matrix products  43.1 us (46%)
  local copies, waits for them, and re-layouts  25.4 us (27%)
  waiting for transfers between devices  11.4 us (12%)
  starting transfers between devices  8.89 us (10%)
  other arithmetic  3.51 us (4%)
    dot_general x2, matrix products, gcn_layer(): jnp.dot(adj_int, layer_in, preferred_element_type=jnp.float32)  24.8 us
    dot_general x2, matrix products, gcn_layer(): jnp.dot(agg_sum.astype(jnp.bfloat16), weight, preferred_element_type=jnp....  18.3 us
    gather x4, local copies, waits for them, and re-layouts, gcn_layer(): sent_rows = jnp.take(layer_in, send_idx, axis=0)  16.3 us
    ppermute x2, waiting for transfers between devices, gcn_layer(): from_south = lax.ppermute(sent_rows[2], 'tiley', shift_pairs(grid_y, 1))  11.4 us
    unnamed x6, local copies, waits for them, and re-layouts  8.57 us
    ppermute x2, starting transfers between devices, gcn_layer(): from_north = lax.ppermute(sent_rows[3], 'tiley', shift_pairs(grid_y, -1))  4.56 us
    ppermute x2, starting transfers between devices, gcn_layer(): from_east = lax.ppermute(sent_rows[1], 'tilex', shift_pairs(grid_x, -1))  2.46 us
    select_n x2, other arithmetic, gcn_layer(): sent_rows = jnp.take(layer_in, send_idx, axis=0)  2.12 us
  transfers between devices with their start and end apart: 8, of which 1 were waited for; matrix products, arithmetic and copies ran while one was open for 27% of the time, Pallas kernels for 0%

commit v1 on v0

v1 whole, which is shorter than its diff:
```python
import functools

import jax
import jax.numpy as jnp
from jax import lax
from jax.experimental import pallas as pl
from jax.experimental.pallas import tpu as pltpu
from jax.sharding import PartitionSpec as P

BF16 = jnp.bfloat16
F32 = jnp.float32
MESH = pl.DeviceIdType.MESH
N_TILE = 256
NN = (((1,), (0,)), ((), ()))
NT = (((1,), (1,)), ((), ()))


def dot(lhs, rhs, dims):
    return lax.dot_general(lhs, rhs, dims, preferred_element_type=F32)


def feature_chunks(feat):
    cuts = [0, 128]
    while feat - cuts[-1] > 512:
        cuts.append(cuts[-1] + 256)
    if feat - cuts[-1] > 256:
        cuts.append(cuts[-1] + 128)
    cuts.append(feat)
    return list(zip(cuts[:-1], cuts[1:]))


def gcn_kernel(grid_y, grid_x, chunks, idx_ref, w0_ref, w1_ref, feat_hbm, int_hbm, halo_hbm, out_ref,
               feat_v, int_v, halo_v, pick_v, send_y, send_x0, send_x1, recv_y, recv_x, z_int, hid_acc,
               hid_v, send2_y, send2_x0, send2_x1, recv2_y, recv2_x,
               feat_sem, int_sem, halo_sem, sy_sem, ry_sem, sx_sem, rx_sem, s2_sem, r2_sem):
    me_y = lax.axis_index('tiley')
    me_x = lax.axis_index('tilex')
    east = {'tilex': lax.rem(me_x + 1, grid_x)}
    west = {'tilex': lax.rem(me_x + grid_x - 1, grid_x)}
    north = {'tiley': lax.rem(me_y + 1, grid_y)}
    nodes = int_v.shape[0]
    half = halo_v.shape[1] // 2
    quarter = half // 2

    feat_in = []
    for num, (lo, hi) in enumerate(chunks):
        rows = pl.ds(lo, hi - lo)
        feat_in.append(pltpu.make_async_copy(feat_hbm.at[rows, :], feat_v.at[rows, :], feat_sem.at[num]))
        feat_in[-1].start()
    int_in = pltpu.make_async_copy(int_hbm, int_v, int_sem)
    int_in.start()
    halo_in = pltpu.make_async_copy(halo_hbm, halo_v, halo_sem)
    halo_in.start()

    barrier = pltpu.get_barrier_semaphore()
    for neighbour in (north, east, west):
        pl.semaphore_signal(barrier, inc=1, device_id=neighbour, device_id_type=MESH)

    def build_pick(first_buf):
        for buf in (first_buf, first_buf + 1):
            plan = idx_ref[buf:buf + 1, :]

            @pl.loop(0, nodes // N_TILE)
            def _(blk):
                start = pl.multiple_of(blk * N_TILE, N_TILE)
                node_ids = lax.broadcasted_iota(jnp.int32, (N_TILE, quarter), 0) + start
                pick_v[pl.ds(start, N_TILE), buf * quarter:(buf + 1) * quarter] = jnp.where(node_ids == plan, 1.0, 0.0).astype(BF16)

    def remote(src, dst, send_sem, recv_sem, target):
        return pltpu.make_async_remote_copy(src_ref=src, dst_ref=dst, send_sem=send_sem, recv_sem=recv_sem, device_id=target, device_id_type=MESH)

    build_pick(2)
    y_copies = []
    for num, (lo, hi) in enumerate(chunks):
        rows = pl.ds(lo, hi - lo)
        feat_in[num].wait()
        send_y[rows, :] = dot(feat_v[rows, :], pick_v[:, half:], NN).astype(BF16)
        if num == 0:
            pl.semaphore_wait(barrier, 3)
        y_copies.append(remote(send_y.at[rows, :], recv_y.at[rows, :], sy_sem.at[num], ry_sem.at[num], north))
        y_copies[-1].start()
    build_pick(0)
    x_copies = []
    for num, (lo, hi) in enumerate(chunks):
        rows = pl.ds(lo, hi - lo)
        picked = dot(feat_v[rows, :], pick_v[:, :half], NN).astype(BF16)
        send_x0[rows, :] = picked[:, :quarter]
        send_x1[rows, :] = picked[:, quarter:]
        x_copies.append(remote(send_x0.at[rows, :], recv_x.at[rows, :quarter], sx_sem.at[2 * num], rx_sem.at[2 * num], east))
        x_copies.append(remote(send_x1.at[rows, :], recv_x.at[rows, quarter:], sx_sem.at[2 * num + 1], rx_sem.at[2 * num + 1], west))
        x_copies[-2].start()
        x_copies[-1].start()

    int_in.wait()

    @pl.loop(0, nodes // N_TILE)
    def _(blk):
        cols = pl.ds(pl.multiple_of(blk * N_TILE, N_TILE), N_TILE)
        for lo, hi in chunks:
            rows = pl.ds(lo, hi - lo)
            z_int[rows, cols] = dot(feat_v[rows, :], int_v[cols, :], NT)

    halo_in.wait()
    for copy in x_copies:
        copy.wait_recv()

    @pl.loop(0, nodes // N_TILE)
    def _(blk):
        cols = pl.ds(pl.multiple_of(blk * N_TILE, N_TILE), N_TILE)
        for lo, hi in chunks:
            rows = pl.ds(lo, hi - lo)
            z_int[rows, cols] += dot(recv_x[rows, :], halo_v[cols, :half], NT)

    for num, (lo, hi) in enumerate(chunks):
        rows = pl.ds(lo, hi - lo)
        y_copies[num].wait_recv()

        @pl.loop(0, nodes // N_TILE)
        def _(blk):
            cols = pl.ds(pl.multiple_of(blk * N_TILE, N_TILE), N_TILE)
            z_sum = (z_int[rows, cols] + dot(recv_y[rows, :], halo_v[cols, half:], NT)).astype(BF16)
            part = dot(w0_ref[:, lo:hi], z_sum, NN)
            if num == 0:
                hid_acc[:, cols] = part
            else:
                hid_acc[:, cols] += part

    hid_v[...] = jnp.maximum(hid_acc[...], 0.0).astype(BF16)
    hidden = hid_v[...]
    send2_y[...] = dot(hidden, pick_v[:, half:], NN).astype(BF16)
    picked = dot(hidden, pick_v[:, :half], NN).astype(BF16)
    send2_x0[...] = picked[:, :quarter]
    send2_x1[...] = picked[:, quarter:]
    second = [
        remote(send2_y, recv2_y, s2_sem.at[0], r2_sem.at[0], north),
        remote(send2_x0, recv2_x.at[:, :quarter], s2_sem.at[1], r2_sem.at[1], east),
        remote(send2_x1, recv2_x.at[:, quarter:], s2_sem.at[2], r2_sem.at[2], west),
    ]
    for copy in second:
        copy.start()

    @pl.loop(0, nodes // N_TILE)
    def _(blk):
        cols = pl.ds(pl.multiple_of(blk * N_TILE, N_TILE), N_TILE)
        hid_acc[:, cols] = dot(hid_v[...], int_v[cols, :], NT)

    for copy in second:
        copy.wait_recv()

    @pl.loop(0, nodes // N_TILE)
    def _(blk):
        cols = pl.ds(pl.multiple_of(blk * N_TILE, N_TILE), N_TILE)
        z_sum = hid_acc[:, cols] + (dot(recv2_x[...], halo_v[cols, :half], NT) + dot(recv2_y[...], halo_v[cols, half:], NT))
        out_ref[:, cols] = dot(w1_ref[...], z_sum.astype(BF16), NN).astype(BF16)

    for copy in y_copies + x_copies + second:
        copy.wait_send()


def solution(mesh):
    grid_y = mesh.shape['tiley']
    grid_x = mesh.shape['tilex']
    node_spec = P(('parts', 'tiley', 'tilex'), None)
    full_spec = P(None, None)

    def per_device(node_feats, adj_int, adj_halo, send_idx, w_hidden, w_out):
        nodes, feat = node_feats.shape
        slots = adj_halo.shape[1]
        half, quarter = slots // 2, slots // 4
        hidden, classes = w_out.shape
        chunks = feature_chunks(feat)
        vmem = pl.BlockSpec(memory_space=pltpu.VMEM)
        hbm = pl.BlockSpec(memory_space=pl.ANY)
        dma = pltpu.SemaphoreType.DMA
        out = pl.pallas_call(
            functools.partial(gcn_kernel, grid_y, grid_x, chunks),
            out_shape=jax.ShapeDtypeStruct((classes, nodes), BF16),
            in_specs=[vmem, vmem, vmem, hbm, hbm, hbm],
            out_specs=vmem,
            scratch_shapes=[
                pltpu.VMEM((feat, nodes), BF16),
                pltpu.VMEM((nodes, nodes), BF16),
                pltpu.VMEM((nodes, slots), BF16),
                pltpu.VMEM((nodes, slots), BF16),
                pltpu.VMEM((feat, half), BF16),
                pltpu.VMEM((feat, quarter), BF16),
                pltpu.VMEM((feat, quarter), BF16),
                pltpu.VMEM((feat, half), BF16),
                pltpu.VMEM((feat, half), BF16),
                pltpu.VMEM((feat, nodes), F32),
                pltpu.VMEM((hidden, nodes), F32),
                pltpu.VMEM((hidden, nodes), BF16),
                pltpu.VMEM((hidden, half), BF16),
                pltpu.VMEM((hidden, quarter), BF16),
                pltpu.VMEM((hidden, quarter), BF16),
                pltpu.VMEM((hidden, half), BF16),
                pltpu.VMEM((hidden, half), BF16),
                dma((len(chunks),)),
                dma,
                dma,
                dma((len(chunks),)),
                dma((len(chunks),)),
                dma((2 * len(chunks),)),
                dma((2 * len(chunks),)),
                dma((3,)),
                dma((3,)),
            ],
            compiler_params=pltpu.CompilerParams(collective_id=0, has_side_effects=True, vmem_limit_bytes=60 * 2**20),
        )(send_idx, w_hidden.T, w_out.T, node_feats.T, adj_int, adj_halo)
        return out.T

    return jax.shard_map(per_device, mesh=mesh, in_specs=(node_spec, node_spec, node_spec, node_spec, full_spec, full_spec), out_specs=node_spec, check_vma=False)
```

time: 92.9 us -> 66.6 us (0.72)
  Pallas kernels: 0 us -> 65 us
  matrix products: 43.1 us -> 0 us
  local copies, waits for them, and re-layouts: 25.4 us -> 1.38 us
  waiting for transfers between devices: 11.4 us -> 0 us
  starting transfers between devices: 8.89 us -> 0 us
  other arithmetic: 3.51 us -> 0 us
    pallas_call x0 -> x1, Pallas kernels: none -> 65 us  [per_device(): pl.pallas_call(functools.partial(gcn_kernel, grid_y, grid_x, chunks), out...]
    dot_general x4 -> x0, matrix products: 43.1 us -> none  [the longest x2 24.8 us: gcn_layer(): jnp.dot(adj_int, layer_in, preferred_element_type=jnp.float32)]
    gather x4 -> x0, local copies, waits for them, and re-layouts: 16.3 us -> none  [gcn_layer(): sent_rows = jnp.take(layer_in, send_idx, axis=0)]
    ppermute x8 -> x0, waiting for transfers between devices: 11.4 us -> none  [the longest x2 11.4 us: gcn_layer(): from_south = lax.ppermute(sent_rows[2], 'tiley', shift_pairs(grid_y, 1))]
    ppermute x8 -> x0, starting transfers between devices: 8.89 us -> none  [the longest x2 4.56 us: gcn_layer(): from_north = lax.ppermute(sent_rows[3], 'tiley', shift_pairs(grid_y, -1))]
    unnamed x6 -> x1, local copies, waits for them, and re-layouts: 8.57 us -> 1.38 us
    select_n x2 -> x0, other arithmetic: 2.12 us -> none  [gcn_layer(): sent_rows = jnp.take(layer_in, send_idx, axis=0)]
  transfers between devices with their start and end apart: 8 -> 0, of which waited for: 1 -> 0; matrix products, arithmetic and copies ran while one was open for 27% -> 0% of each run, Pallas kernels for 0% -> 0%
where the time goes in v1:
time: 66.6 us; the launch traced here: 66.4 us
  Pallas kernels  65 us (98%)
  local copies, waits for them, and re-layouts  1.38 us (2%)
    pallas_call x1, Pallas kernels, per_device(): pl.pallas_call(functools.partial(gcn_kernel, grid_y, grid_x, chunks), out...  65 us
    unnamed x1, local copies, waits for them, and re-layouts  1.38 us

profile of v1, /device:TPU:0, one launch (start us, length us, event | category | flops | bytes accessed | tf_op | source)
XLA Modules:
  0.0 66.4 jit_solution(7867635211331809124)
XLA Ops:
  0.0 65.0 %shard_map.64 = bf16[7,2048]{1,0:T(8,128)(2,1)} custom-call(s32[4,256]{1,0:T(4,128)} %idx_ref.1, bf16[16,1433]{1,0:T(8,128)(2,1)} %bitcast.6, bf16[7,16]{1,0:T(8,128)(2,1)} %bitcast.7, bf16[1433,2048]{1,0:T(8,128)(2,1)} %bitcast.4, bf16[2048,2048]{1,0:T(8,128)(2,1)} %int_hbm.1, bf16[2048,1024]{1,0:T(8,128)(2,1)} %halo_hbm.1), custom_call_target="tpu_custom_call" | custom-call | tf_op jit(solution)/shard_map/pallas_call | solution.py:175
  65.0 1.4 %copy.8 = bf16[2048,7]{0,1:T(8,128)(2,1)} copy(bf16[2048,7]{0,1:T(8,128)(2,1)} %bitcast.5) | data formatting | bytes 57344

commit v2 on v1

--- a/solution.py
+++ b/solution.py
@@ -11,6 +11,9 @@
 F32 = jnp.float32
 MESH = pl.DeviceIdType.MESH
 N_TILE = 256
+BIG_ROWS = 512
+BIG_COLS = 1024
+HALO_COLS = 512
 NN = (((1,), (0,)), ((), ()))
 NT = (((1,), (1,)), ((), ()))
 
@@ -30,7 +33,7 @@
 
 
 def gcn_kernel(grid_y, grid_x, chunks, idx_ref, w0_ref, w1_ref, feat_hbm, int_hbm, halo_hbm, out_ref,
-               feat_v, int_v, halo_v, pick_v, send_y, send_x0, send_x1, recv_y, recv_x, z_int, hid_acc,
+               feat_v, int_v, halo_v, pick_v, send_y, send_x0, send_x1, recv_y, recv_x, z_int, z_half, hid_acc,
                hid_v, send2_y, send2_x0, send2_x1, recv2_y, recv2_x,
                feat_sem, int_sem, halo_sem, sy_sem, ry_sem, sx_sem, rx_sem, s2_sem, r2_sem):
     me_y = lax.axis_index('tiley')
@@ -69,92 +72,103 @@
     def remote(src, dst, send_sem, recv_sem, target):
         return pltpu.make_async_remote_copy(src_ref=src, dst_ref=dst, send_sem=send_sem, recv_sem=recv_sem, device_id=target, device_id_type=MESH)
 
-    build_pick(2)
+    with jax.named_scope('pick_y'):
+        build_pick(2)
     y_copies = []
-    for num, (lo, hi) in enumerate(chunks):
-        rows = pl.ds(lo, hi - lo)
-        feat_in[num].wait()
-        send_y[rows, :] = dot(feat_v[rows, :], pick_v[:, half:], NN).astype(BF16)
-        if num == 0:
-            pl.semaphore_wait(barrier, 3)
+    x_copies = []
+
+    def send_y_rows(num, rows):
         y_copies.append(remote(send_y.at[rows, :], recv_y.at[rows, :], sy_sem.at[num], ry_sem.at[num], north))
         y_copies[-1].start()
-    build_pick(0)
-    x_copies = []
-    for num, (lo, hi) in enumerate(chunks):
-        rows = pl.ds(lo, hi - lo)
-        picked = dot(feat_v[rows, :], pick_v[:, :half], NN).astype(BF16)
-        send_x0[rows, :] = picked[:, :quarter]
-        send_x1[rows, :] = picked[:, quarter:]
+
+    def send_x_rows(num, rows):
         x_copies.append(remote(send_x0.at[rows, :], recv_x.at[rows, :quarter], sx_sem.at[2 * num], rx_sem.at[2 * num], east))
         x_copies.append(remote(send_x1.at[rows, :], recv_x.at[rows, quarter:], sx_sem.at[2 * num + 1], rx_sem.at[2 * num + 1], west))
         x_copies[-2].start()
         x_copies[-1].start()
 
-    int_in.wait()
-
-    @pl.loop(0, nodes // N_TILE)
-    def _(blk):
-        cols = pl.ds(pl.multiple_of(blk * N_TILE, N_TILE), N_TILE)
-        for lo, hi in chunks:
-            rows = pl.ds(lo, hi - lo)
-            z_int[rows, cols] = dot(feat_v[rows, :], int_v[cols, :], NT)
-
-    halo_in.wait()
-    for copy in x_copies:
-        copy.wait_recv()
-
-    @pl.loop(0, nodes // N_TILE)
-    def _(blk):
-        cols = pl.ds(pl.multiple_of(blk * N_TILE, N_TILE), N_TILE)
-        for lo, hi in chunks:
-            rows = pl.ds(lo, hi - lo)
-            z_int[rows, cols] += dot(recv_x[rows, :], halo_v[cols, :half], NT)
-
     for num, (lo, hi) in enumerate(chunks):
         rows = pl.ds(lo, hi - lo)
-        y_copies[num].wait_recv()
-
-        @pl.loop(0, nodes // N_TILE)
+        with jax.named_scope(f'feat_wait{num}'):
+            feat_in[num].wait()
+        with jax.named_scope(f'gather_y{num}'):
+            send_y[rows, :] = dot(feat_v[rows, :], pick_v[:, half:], NN).astype(BF16)
+        if num == 0:
+            with jax.named_scope('barrier'):
+                pl.semaphore_wait(barrier, 3)
+        send_y_rows(num, rows)
+        if num == 0:
+            with jax.named_scope('pick_x'):
+                build_pick(0)
+        with jax.named_scope(f'gather_x{num}'):
+            picked = dot(feat_v[rows, :], pick_v[:, :half], NN).astype(BF16)
+            send_x0[rows, :] = picked[:, :quarter]
+            send_x1[rows, :] = picked[:, quarter:]
+        send_x_rows(num, rows)
+
+    with jax.named_scope('int_wait'):
+        int_in.wait()
+    big = [(lo, min(lo + BIG_ROWS, feat_v.shape[0])) for lo in range(0, feat_v.shape[0], BIG_ROWS)]
+    with jax.named_scope('interior'):
+
+        @pl.loop(0, nodes // BIG_COLS)
         def _(blk):
-            cols = pl.ds(pl.multiple_of(blk * N_TILE, N_TILE), N_TILE)
-            z_sum = (z_int[rows, cols] + dot(recv_y[rows, :], halo_v[cols, half:], NT)).astype(BF16)
-            part = dot(w0_ref[:, lo:hi], z_sum, NN)
+            cols = pl.ds(pl.multiple_of(blk * BIG_COLS, BIG_COLS), BIG_COLS)
+            for lo, hi in big:
+                z_int[lo:hi, cols] = dot(feat_v[lo:hi, :], int_v[cols, :], NT)
+
+    with jax.named_scope('xwait'):
+        halo_in.wait()
+        for copy in x_copies:
+            copy.wait_recv()
+    with jax.named_scope('xhalo'):
+
+        @pl.loop(0, nodes // BIG_COLS)
+        def _(blk):
+            cols = pl.ds(pl.multiple_of(blk * BIG_COLS, BIG_COLS), BIG_COLS)
+            for lo, hi in big:
+                z_int[lo:hi, cols] += dot(recv_x[lo:hi, :], halo_v[cols, :half], NT)
+
+    for num, (lo, hi) in enumerate(chunks):
+        rows = pl.ds(lo, hi - lo)
+        with jax.named_scope(f'ywait{num}'):
+            y_copies[num].wait_recv()
+        with jax.named_scope(f'yhalo{num}'):
+            for col in range(0, nodes, HALO_COLS):
+                cols = pl.ds(col, HALO_COLS)
+                z_half[rows, cols] = (z_int[rows, cols] + dot(recv_y[rows, :], halo_v[cols, half:], NT)).astype(BF16)
+            part = dot(w0_ref[:, lo:hi], z_half[rows, :], NN)
             if num == 0:
-                hid_acc[:, cols] = part
+                hid_acc[...] = part
             else:
-                hid_acc[:, cols] += part
-
-    hid_v[...] = jnp.maximum(hid_acc[...], 0.0).astype(BF16)
-    hidden = hid_v[...]
-    send2_y[...] = dot(hidden, pick_v[:, half:], NN).astype(BF16)
-    picked = dot(hidden, pick_v[:, :half], NN).astype(BF16)
-    send2_x0[...] = picked[:, :quarter]
-    send2_x1[...] = picked[:, quarter:]
-    second = [
-        remote(send2_y, recv2_y, s2_sem.at[0], r2_sem.at[0], north),
-        remote(send2_x0, recv2_x.at[:, :quarter], s2_sem.at[1], r2_sem.at[1], east),
-        remote(send2_x1, recv2_x.at[:, quarter:], s2_sem.at[2], r2_sem.at[2], west),
-    ]
-    for copy in second:
-        copy.start()
-
-    @pl.loop(0, nodes // N_TILE)
-    def _(blk):
-        cols = pl.ds(pl.multiple_of(blk * N_TILE, N_TILE), N_TILE)
-        hid_acc[:, cols] = dot(hid_v[...], int_v[cols, :], NT)
-
-    for copy in second:
-        copy.wait_recv()
-
-    @pl.loop(0, nodes // N_TILE)
-    def _(blk):
-        cols = pl.ds(pl.multiple_of(blk * N_TILE, N_TILE), N_TILE)
-        z_sum = hid_acc[:, cols] + (dot(recv2_x[...], halo_v[cols, :half], NT) + dot(recv2_y[...], halo_v[cols, half:], NT))
-        out_ref[:, cols] = dot(w1_ref[...], z_sum.astype(BF16), NN).astype(BF16)
-
-    for copy in y_copies + x_copies + second:
-        copy.wait_send()
+                hid_acc[...] += part
+
+    with jax.named_scope('gather2'):
+        hidden = jnp.maximum(hid_acc[...], 0.0).astype(BF16)
+        hid_v[...] = hidden
+        send2_y[...] = dot(hidden, pick_v[:, half:], NN).astype(BF16)
+        picked = dot(hidden, pick_v[:, :half], NN).astype(BF16)
+        send2_x0[...] = picked[:, :quarter]
+        send2_x1[...] = picked[:, quarter:]
+        second = [
+            remote(send2_y, recv2_y, s2_sem.at[0], r2_sem.at[0], north),
+            remote(send2_x0, recv2_x.at[:, :quarter], s2_sem.at[1], r2_sem.at[1], east),
+            remote(send2_x1, recv2_x.at[:, quarter:], s2_sem.at[2], r2_sem.at[2], west),
+        ]
+        for copy in second:
+            copy.start()
+
+    with jax.named_scope('interior2'):
+        hid_acc[...] = dot(hid_v[...], int_v[...], NT)
+    with jax.named_scope('wait2'):
+        for copy in second:
+            copy.wait_recv()
+    with jax.named_scope('halo2'):
+        z_sum = hid_acc[...] + (dot(recv2_x[...], halo_v[:, :half], NT) + dot(recv2_y[...], halo_v[:, half:], NT))
+        out_ref[...] = dot(w1_ref[...], z_sum.astype(BF16), NN).astype(BF16)
+    with jax.named_scope('sendwait'):
+        for copy in y_copies + x_copies + second:
+            copy.wait_send()
 
 
 def solution(mesh):
@@ -188,6 +202,7 @@
                 pltpu.VMEM((feat, half), BF16),
                 pltpu.VMEM((feat, half), BF16),
                 pltpu.VMEM((feat, nodes), F32),
+                pltpu.VMEM((feat, nodes), BF16),
                 pltpu.VMEM((hidden, nodes), F32),
                 pltpu.VMEM((hidden, nodes), BF16),
                 pltpu.VMEM((hidden, half), BF16),

time: 66.6 us -> 46 us (0.69)
  Pallas kernels: 65 us -> 44.4 us
    pallas_call x1, Pallas kernels: 65 us -> 44.4 us  [per_device(): pl.pallas_call(functools.partial(gcn_kernel, grid_y, grid_x, chunks), out...]
where the time goes in v2:
time: 46 us; the launch traced here: 45.8 us
  Pallas kernels  44.4 us (97%)
  local copies, waits for them, and re-layouts  1.38 us (3%)
    pallas_call x1, Pallas kernels, per_device(): pl.pallas_call(functools.partial(gcn_kernel, grid_y, grid_x, chunks), out...  44.4 us
    unnamed x1, local copies, waits for them, and re-layouts  1.38 us

profile of v2, /device:TPU:0, one launch (start us, length us, event | category | flops | bytes accessed | tf_op | source)
XLA Modules:
  0.0 45.8 jit_solution(1383238049650931233)
XLA Ops:
  0.0 44.4 %shard_map.64 = bf16[7,2048]{1,0:T(8,128)(2,1)} custom-call(s32[4,256]{1,0:T(4,128)} %idx_ref.1, bf16[16,1433]{1,0:T(8,128)(2,1)} %bitcast.6, bf16[7,16]{1,0:T(8,128)(2,1)} %bitcast.7, bf16[1433,2048]{1,0:T(8,128)(2,1)} %bitcast.4, bf16[2048,2048]{1,0:T(8,128)(2,1)} %int_hbm.1, bf16[2048,1024]{1,0:T(8,128)(2,1)} %halo_hbm.1), custom_call_target="tpu_custom_call" | custom-call | tf_op jit(solution)/shard_map/pallas_call | solution.py:189
  44.4 1.4 %copy.8 = bf16[2048,7]{0,1:T(8,128)(2,1)} copy(bf16[2048,7]{0,1:T(8,128)(2,1)} %bitcast.5) | data formatting | bytes 57344

commit v3 on v2

--- a/solution.py
+++ b/solution.py
@@ -32,10 +32,10 @@
     return list(zip(cuts[:-1], cuts[1:]))
 
 
-def gcn_kernel(grid_y, grid_x, chunks, idx_ref, w0_ref, w1_ref, feat_hbm, int_hbm, halo_hbm, out_ref,
-               feat_v, int_v, halo_v, pick_v, send_y, send_x0, send_x1, recv_y, recv_x, z_int, z_half, hid_acc,
+def gcn_kernel(grid_y, grid_x, chunks, idx_hbm, w0_hbm, w1_hbm, feat_hbm, int_hbm, halo_hbm, out_ref,
+               idx_ref, w0_ref, w1_ref, feat_v, int_v, halo_v, halo_t, pick_v, send_y, send_x0, send_x1, recv_y, recv_x, z_int, z_half, hid_acc,
                hid_v, send2_y, send2_x0, send2_x1, recv2_y, recv2_x,
-               feat_sem, int_sem, halo_sem, sy_sem, ry_sem, sx_sem, rx_sem, s2_sem, r2_sem):
+               small_sem, feat_sem, int_sem, halo_sem, sy_sem, ry_sem, sx_sem, rx_sem, s2_sem, r2_sem):
     me_y = lax.axis_index('tiley')
     me_x = lax.axis_index('tilex')
     east = {'tilex': lax.rem(me_x + 1, grid_x)}
@@ -45,35 +45,41 @@
     half = halo_v.shape[1] // 2
     quarter = half // 2
 
+    barrier = pltpu.get_barrier_semaphore()
+    for neighbour in (north, east, west):
+        pl.semaphore_signal(barrier, inc=1, device_id=neighbour, device_id_type=MESH)
+
+    idx_in = pltpu.make_async_copy(idx_hbm, idx_ref, small_sem.at[0])
     feat_in = []
     for num, (lo, hi) in enumerate(chunks):
         rows = pl.ds(lo, hi - lo)
         feat_in.append(pltpu.make_async_copy(feat_hbm.at[rows, :], feat_v.at[rows, :], feat_sem.at[num]))
-        feat_in[-1].start()
+    w0_in = pltpu.make_async_copy(w0_hbm, w0_ref, small_sem.at[1])
+    w1_in = pltpu.make_async_copy(w1_hbm, w1_ref, small_sem.at[2])
     int_in = pltpu.make_async_copy(int_hbm, int_v, int_sem)
-    int_in.start()
     halo_in = pltpu.make_async_copy(halo_hbm, halo_v, halo_sem)
-    halo_in.start()
-
-    barrier = pltpu.get_barrier_semaphore()
-    for neighbour in (north, east, west):
-        pl.semaphore_signal(barrier, inc=1, device_id=neighbour, device_id_type=MESH)
+    idx_in.start()
+    feat_in[0].start()
+
+    def pick_block(buf, start):
+        node_ids = lax.broadcasted_iota(jnp.int32, (N_TILE, quarter), 0) + start
+        return jnp.where(node_ids == idx_ref[buf:buf + 1, :], 1.0, 0.0).astype(BF16)
 
     def build_pick(first_buf):
         for buf in (first_buf, first_buf + 1):
-            plan = idx_ref[buf:buf + 1, :]
 
             @pl.loop(0, nodes // N_TILE)
             def _(blk):
                 start = pl.multiple_of(blk * N_TILE, N_TILE)
-                node_ids = lax.broadcasted_iota(jnp.int32, (N_TILE, quarter), 0) + start
-                pick_v[pl.ds(start, N_TILE), buf * quarter:(buf + 1) * quarter] = jnp.where(node_ids == plan, 1.0, 0.0).astype(BF16)
+                pick_v[pl.ds(start, N_TILE), buf * quarter:(buf + 1) * quarter] = pick_block(buf, start)
 
     def remote(src, dst, send_sem, recv_sem, target):
         return pltpu.make_async_remote_copy(src_ref=src, dst_ref=dst, send_sem=send_sem, recv_sem=recv_sem, device_id=target, device_id_type=MESH)
 
-    with jax.named_scope('pick_y'):
-        build_pick(2)
+    with jax.named_scope('idx_wait'):
+        idx_in.wait()
+    for copy in feat_in[1:]:
+        copy.start()
     y_copies = []
     x_copies = []
 
@@ -92,12 +98,23 @@
         with jax.named_scope(f'feat_wait{num}'):
             feat_in[num].wait()
         with jax.named_scope(f'gather_y{num}'):
-            send_y[rows, :] = dot(feat_v[rows, :], pick_v[:, half:], NN).astype(BF16)
+            if num == 0:
+                picked = None
+                for start in range(0, nodes, N_TILE):
+                    block = jnp.concatenate([pick_block(2, start), pick_block(3, start)], axis=1)
+                    pick_v[start:start + N_TILE, half:] = block
+                    part = dot(feat_v[rows, start:start + N_TILE], block, NN)
+                    picked = part if picked is None else picked + part
+                send_y[rows, :] = picked.astype(BF16)
+            else:
+                send_y[rows, :] = dot(feat_v[rows, :], pick_v[:, half:], NN).astype(BF16)
         if num == 0:
             with jax.named_scope('barrier'):
                 pl.semaphore_wait(barrier, 3)
         send_y_rows(num, rows)
         if num == 0:
+            for copy in (int_in, halo_in, w0_in, w1_in):
+                copy.start()
             with jax.named_scope('pick_x'):
                 build_pick(0)
         with jax.named_scope(f'gather_x{num}'):
@@ -108,17 +125,20 @@
 
     with jax.named_scope('int_wait'):
         int_in.wait()
+        halo_in.wait()
+        w0_in.wait()
+        w1_in.wait()
     big = [(lo, min(lo + BIG_ROWS, feat_v.shape[0])) for lo in range(0, feat_v.shape[0], BIG_ROWS)]
     with jax.named_scope('interior'):
 
         @pl.loop(0, nodes // BIG_COLS)
         def _(blk):
             cols = pl.ds(pl.multiple_of(blk * BIG_COLS, BIG_COLS), BIG_COLS)
+            halo_t[:, cols] = halo_v[cols, :].T
             for lo, hi in big:
                 z_int[lo:hi, cols] = dot(feat_v[lo:hi, :], int_v[cols, :], NT)
 
     with jax.named_scope('xwait'):
-        halo_in.wait()
         for copy in x_copies:
             copy.wait_recv()
     with jax.named_scope('xhalo'):
@@ -136,7 +156,7 @@
         with jax.named_scope(f'yhalo{num}'):
             for col in range(0, nodes, HALO_COLS):
                 cols = pl.ds(col, HALO_COLS)
-                z_half[rows, cols] = (z_int[rows, cols] + dot(recv_y[rows, :], halo_v[cols, half:], NT)).astype(BF16)
+                z_half[rows, cols] = (z_int[rows, cols] + dot(recv_y[rows, :], halo_t[half:, cols], NN)).astype(BF16)
             part = dot(w0_ref[:, lo:hi], z_half[rows, :], NN)
             if num == 0:
                 hid_acc[...] = part
@@ -164,7 +184,7 @@
         for copy in second:
             copy.wait_recv()
     with jax.named_scope('halo2'):
-        z_sum = hid_acc[...] + (dot(recv2_x[...], halo_v[:, :half], NT) + dot(recv2_y[...], halo_v[:, half:], NT))
+        z_sum = hid_acc[...] + (dot(recv2_x[...], halo_t[:half, :], NN) + dot(recv2_y[...], halo_t[half:, :], NN))
         out_ref[...] = dot(w1_ref[...], z_sum.astype(BF16), NN).astype(BF16)
     with jax.named_scope('sendwait'):
         for copy in y_copies + x_copies + second:
@@ -188,13 +208,17 @@
         dma = pltpu.SemaphoreType.DMA
         out = pl.pallas_call(
             functools.partial(gcn_kernel, grid_y, grid_x, chunks),
-            out_shape=jax.ShapeDtypeStruct((classes, nodes), BF16),
-            in_specs=[vmem, vmem, vmem, hbm, hbm, hbm],
+            out_shape=pltpu.VMEM((classes, nodes), BF16),
+            in_specs=[hbm] * 6,
             out_specs=vmem,
             scratch_shapes=[
+                pltpu.VMEM(send_idx.shape, jnp.int32),
+                pltpu.VMEM((hidden, feat), BF16),
+                pltpu.VMEM((classes, hidden), BF16),
                 pltpu.VMEM((feat, nodes), BF16),
                 pltpu.VMEM((nodes, nodes), BF16),
                 pltpu.VMEM((nodes, slots), BF16),
+                pltpu.VMEM((slots, nodes), BF16),
                 pltpu.VMEM((nodes, slots), BF16),
                 pltpu.VMEM((feat, half), BF16),
                 pltpu.VMEM((feat, quarter), BF16),
@@ -210,6 +234,7 @@
                 pltpu.VMEM((hidden, quarter), BF16),
                 pltpu.VMEM((hidden, half), BF16),
                 pltpu.VMEM((hidden, half), BF16),
+                dma((3,)),
                 dma((len(chunks),)),
                 dma,
                 dma,

time: 46 us -> 42.9 us (0.933)
  Pallas kernels: 44.4 us -> 42.2 us
  local copies, waits for them, and re-layouts: 1.38 us -> 0.62 us
    pallas_call x1, Pallas kernels: 44.4 us -> 42.2 us  [per_device(): pl.pallas_call(functools.partial(gcn_kernel, grid_y, grid_x, chunks), out...]
    unnamed x1, local copies, waits for them, and re-layouts: 1.38 us -> 0.62 us
where the time goes in v3:
time: 42.9 us; the launch traced here: 42.8 us
  Pallas kernels  42.2 us (98%)
  local copies, waits for them, and re-layouts  0.62 us (1%)
    pallas_call x1, Pallas kernels, per_device(): pl.pallas_call(functools.partial(gcn_kernel, grid_y, grid_x, chunks), out...  42.2 us

profile of v3, /device:TPU:0, one launch (start us, length us, event | category | flops | bytes accessed | tf_op | source)
XLA Modules:
  0.0 42.8 jit_solution(7801722831043601105)
XLA Ops:
  0.0 42.2 %shard_map.64 = bf16[7,2048]{1,0:T(8,128)(2,1)S(1)} custom-call(s32[4,256]{1,0:T(4,128)} %idx_hbm.1, bf16[16,1433]{1,0:T(8,128)(2,1)} %bitcast.6, bf16[7,16]{1,0:T(8,128)(2,1)} %bitcast.7, bf16[1433,2048]{1,0:T(8,128)(2,1)} %bitcast.5, bf16[2048,2048]{1,0:T(8,128)(2,1)} %int_hbm.1, bf16[2048,1024]{1,0:T(8,128)(2,1)} %halo_hbm.1), custom_call_target="tpu_custom_call" | custom-call | tf_op jit(solution)/shard_map/pallas_call | solution.py:209
  42.2 0.6 %copy.8 = bf16[2048,7]{0,1:T(8,128)(2,1)} copy(bf16[2048,7]{0,1:T(8,128)(2,1)S(1)} %bitcast.4) | data formatting | bytes 57344

commit v4 on v3

v4 whole, which is shorter than its diff:
```python
import functools

import jax
import jax.numpy as jnp
from jax import lax
from jax.experimental import pallas as pl
from jax.experimental.pallas import tpu as pltpu
from jax.sharding import PartitionSpec as P

BF16 = jnp.bfloat16
F32 = jnp.float32
MESH = pl.DeviceIdType.MESH
N_TILE = 256
BIG_ROWS = 512
LAST_ROWS = 96
BIG_COLS = 1024
HALO_COLS = 512
NN = (((1,), (0,)), ((), ()))
NT = (((1,), (1,)), ((), ()))


def dot(lhs, rhs, dims):
    return lax.dot_general(lhs, rhs, dims, preferred_element_type=F32)


def feature_chunks(feat):
    last = (feat - 80) // 64 * 64
    cuts = [0, 64, 256]
    while last - 128 - cuts[-1] > 256:
        cuts.append(cuts[-1] + 256)
    cuts += [last - 128, last, feat]
    return list(zip(cuts[:-1], cuts[1:]))


def big_chunks(feat):
    return [(lo, min(lo + BIG_ROWS, feat)) for lo in range(0, feat, BIG_ROWS)]


def gcn_kernel(grid_y, grid_x, chunks, big, idx_hbm, w0_hbm, w1_hbm, feat_hbm, int_hbm, halo_hbm, out_ref,
               idx_ref, w0_ref, w1_ref, feat_v, int_v, int_t, halo_v, halo_t, pick_v, send_y, send_x0, send_x1, recv_v, z_int, z_half, halo_pick, z_split, z_pick, hid_split, hid_pick, hid_acc,
               hid_v, send2_y, send2_x0, send2_x1, recv2_y, recv2_x,
               small_sem, feat_sem, int_sem, halo_sem, sy_sem, ry_sem, sx_sem, rx_sem, s2_sem, r2_sem):
    me_y = lax.axis_index('tiley')
    me_x = lax.axis_index('tilex')
    east = {'tilex': lax.rem(me_x + 1, grid_x)}
    west = {'tilex': lax.rem(me_x + grid_x - 1, grid_x)}
    north = {'tiley': lax.rem(me_y + 1, grid_y)}
    nodes = int_v.shape[0]
    half = halo_v.shape[1] // 2
    quarter = half // 2
    hid_rows = hid_v.shape[0]

    barrier = pltpu.get_barrier_semaphore()
    for neighbour in (north, east, west):
        pl.semaphore_signal(barrier, inc=1, device_id=neighbour, device_id_type=MESH)

    idx_in = pltpu.make_async_copy(idx_hbm, idx_ref, small_sem.at[0])
    feat_in = []
    for num, (lo, hi) in enumerate(chunks):
        rows = pl.ds(lo, hi - lo)
        feat_in.append(pltpu.make_async_copy(feat_hbm.at[rows, :], feat_v.at[rows, :], feat_sem.at[num]))
    w0_in = pltpu.make_async_copy(w0_hbm, w0_ref, small_sem.at[1])
    w1_in = pltpu.make_async_copy(w1_hbm, w1_ref, small_sem.at[2])
    int_in = pltpu.make_async_copy(int_hbm, int_v, int_sem)
    halo_in = pltpu.make_async_copy(halo_hbm, halo_v, halo_sem)
    idx_in.start()
    feat_in[0].start()

    def pick_block(buf, start):
        node_ids = lax.broadcasted_iota(jnp.int32, (N_TILE, quarter), 0) + start
        return jnp.where(node_ids == idx_ref[buf:buf + 1, :], 1.0, 0.0).astype(BF16)

    def build_pick(first_buf):
        @pl.loop(0, nodes // N_TILE)
        def _(blk):
            start = pl.multiple_of(blk * N_TILE, N_TILE)
            for buf in (first_buf, first_buf + 1):
                pick_v[pl.ds(start, N_TILE), buf * quarter:(buf + 1) * quarter] = pick_block(buf, start)

    def remote(src, dst, send_sem, recv_sem, target):
        return pltpu.make_async_remote_copy(src_ref=src, dst_ref=dst, send_sem=send_sem, recv_sem=recv_sem, device_id=target, device_id_type=MESH)

    with jax.named_scope('idx_wait'):
        idx_in.wait()
    for copy in feat_in[1:]:
        copy.start()
    y_copies = []
    x_copies = []

    def send_y_rows(first, end):
        lo, hi = chunks[first][0], chunks[end - 1][1]
        rows = pl.ds(lo, hi - lo)
        with jax.named_scope(f'feat_wait{first}'):
            for copy in feat_in[first:end]:
                copy.wait()
        with jax.named_scope(f'gather_y{first}'):
            if first == 0:
                picked = None
                for start in range(0, nodes, N_TILE):
                    block = jnp.concatenate([pick_block(2, start), pick_block(3, start)], axis=1)
                    pick_v[start:start + N_TILE, half:] = block
                    part = dot(feat_v[rows, start:start + N_TILE], block, NN)
                    picked = part if picked is None else picked + part
                send_y[rows, :] = picked.astype(BF16)
            else:
                send_y[rows, :] = dot(feat_v[rows, :], pick_v[:, half:], NN).astype(BF16)
        if first == 0:
            with jax.named_scope('barrier'):
                pl.semaphore_wait(barrier, 3)
        for num in range(first, end):
            rows = pl.ds(chunks[num][0], chunks[num][1] - chunks[num][0])
            y_copies.append(remote(send_y.at[rows, :], recv_v.at[rows, half:], sy_sem.at[num], ry_sem.at[num], north))
            y_copies[-1].start()

    def send_x_rows(num):
        rows = pl.ds(big[num][0], big[num][1] - big[num][0])
        with jax.named_scope(f'gather_x{num}'):
            picked = dot(feat_v[rows, :], pick_v[:, :half], NN).astype(BF16)
            send_x0[rows, :] = picked[:, :quarter]
            send_x1[rows, :] = picked[:, quarter:]
        x_copies.append(remote(send_x0.at[rows, :], recv_v.at[rows, :quarter], sx_sem.at[2 * num], rx_sem.at[2 * num], east))
        x_copies.append(remote(send_x1.at[rows, :], recv_v.at[rows, quarter:half], sx_sem.at[2 * num + 1], rx_sem.at[2 * num + 1], west))
        x_copies[-2].start()
        x_copies[-1].start()

    next_x = 0
    for first, end in [(0, 1), (1, 2), (2, 4), (4, len(chunks))]:
        send_y_rows(first, end)
        if first == 0:
            for copy in (int_in, halo_in, w0_in, w1_in):
                copy.start()
        if first == 1:
            with jax.named_scope('pick_x'):
                build_pick(0)
        while next_x < len(big) and big[next_x][1] <= chunks[end - 1][1]:
            send_x_rows(next_x)
            next_x += 1

    with jax.named_scope('int_wait'):
        int_in.wait()
        halo_in.wait()
        w0_in.wait()
        w1_in.wait()
    with jax.named_scope('interior'):

        @pl.loop(0, nodes // BIG_COLS)
        def _(blk):
            cols = pl.ds(pl.multiple_of(blk * BIG_COLS, BIG_COLS), BIG_COLS)
            halo_t[:, cols] = halo_v[cols, :].T
            int_t[:, cols] = int_v[cols, :].T
            for lo, hi in big:
                z_int[lo:hi, cols] = dot(feat_v[lo:hi, :], int_v[cols, :], NT)

    with jax.named_scope('xwait'):
        for copy in x_copies:
            copy.wait_recv()
    def split3(value):
        high = value.astype(BF16)
        rest = value - high.astype(F32)
        middle = rest.astype(BF16)
        return high, middle, (rest - middle.astype(F32)).astype(BF16)

    last_lo, last_hi = chunks[-1]
    last = pl.ds(last_lo, last_hi - last_lo)
    tail = last_hi - last_lo
    with jax.named_scope('halo_pick'):
        halo_pick[...] = dot(halo_t[half:, :], pick_v[...], NN).astype(BF16)
    with jax.named_scope('last_x'):
        z_last = z_int[last, :] + dot(recv_v[last, :half], halo_t[:half, :], NN)
        z_int[last, :] = z_last
        for num, piece in enumerate(split3(z_last)):
            z_split[num * LAST_ROWS:num * LAST_ROWS + tail, :] = piece
    with jax.named_scope('last_pick'):
        parts = dot(z_split[...], pick_v[...], NN)
        z_pick[...] = parts[:LAST_ROWS] + parts[LAST_ROWS:2 * LAST_ROWS] + parts[2 * LAST_ROWS:]

    groups = [(0, 3)] + [(num, num + 1) for num in range(3, len(chunks) - 1)]
    for first, end in groups:
        lo, hi = chunks[first][0], chunks[end - 1][1]
        with jax.named_scope(f'ywait{first}'):
            for copy in y_copies[first:end]:
                copy.wait_recv()
        rows = pl.ds(lo, hi - lo)
        with jax.named_scope(f'yhalo{first}'):
            for col in range(0, nodes, HALO_COLS):
                cols = pl.ds(col, HALO_COLS)
                z_half[:hi - lo, cols] = (z_int[rows, cols] + dot(recv_v[rows, :], halo_t[:, cols], NN)).astype(BF16)
            part = dot(w0_ref[:, lo:hi], z_half[:hi - lo, :], NN)
            if first == 0:
                hid_acc[...] = part
            else:
                hid_acc[...] += part
    with jax.named_scope('hid_pick'):
        for num, piece in enumerate(split3(hid_acc[...])):
            hid_split[num * hid_rows:(num + 1) * hid_rows, :] = piece
        parts = dot(hid_split[...], pick_v[...], NN)
        hid_pick[...] = parts[:hid_rows] + parts[hid_rows:2 * hid_rows] + parts[2 * hid_rows:]

    second = [
        remote(send2_y, recv2_y, s2_sem.at[0], r2_sem.at[0], north),
        remote(send2_x0, recv2_x.at[:, :quarter], s2_sem.at[1], r2_sem.at[1], east),
        remote(send2_x1, recv2_x.at[:, quarter:], s2_sem.at[2], r2_sem.at[2], west),
    ]
    with jax.named_scope('ywait_last'):
        y_copies[-1].wait_recv()
    with jax.named_scope('sent2'):
        z_sent = (z_pick[:tail, :] + dot(recv_v[last, half:], halo_pick[...], NN)).astype(BF16)
        sent = hid_pick[...] + dot(w0_ref[:, last_lo:last_hi], z_sent, NN)
        sent = jnp.maximum(sent, 0.0).astype(BF16)
        send2_y[...] = sent[:, half:]
        send2_x0[...] = sent[:, :quarter]
        send2_x1[...] = sent[:, quarter:half]
    for copy in second:
        copy.start()
    with jax.named_scope('yhalo_last'):
        z_sum = (z_int[last, :] + dot(recv_v[last, half:], halo_t[half:, :], NN)).astype(BF16)
        hid_sum = hid_acc[...] + dot(w0_ref[:, last_lo:last_hi], z_sum, NN)
        hid_v[...] = jnp.maximum(hid_sum, 0.0).astype(BF16)
    with jax.named_scope('interior2'):
        hid_acc[...] = dot(hid_v[...], int_t[...], NN)
    with jax.named_scope('wait2x'):
        second[1].wait_recv()
        second[2].wait_recv()
    with jax.named_scope('xhalo2'):
        hid_acc[...] += dot(recv2_x[...], halo_t[:half, :], NN)
    with jax.named_scope('wait2y'):
        second[0].wait_recv()
    with jax.named_scope('yhalo2'):
        z_sum = hid_acc[...] + dot(recv2_y[...], halo_t[half:, :], NN)
        out_ref[...] = dot(w1_ref[...], z_sum.astype(BF16), NN).astype(BF16)
    with jax.named_scope('sendwait'):
        for copy in y_copies + x_copies + second:
            copy.wait_send()


def solution(mesh):
    grid_y = mesh.shape['tiley']
    grid_x = mesh.shape['tilex']
    node_spec = P(('parts', 'tiley', 'tilex'), None)
    full_spec = P(None, None)

    def per_device(node_feats, adj_int, adj_halo, send_idx, w_hidden, w_out):
        nodes, feat = node_feats.shape
        slots = adj_halo.shape[1]
        half, quarter = slots // 2, slots // 4
        hidden, classes = w_out.shape
        chunks = feature_chunks(feat)
        big = big_chunks(feat)
        vmem = pl.BlockSpec(memory_space=pltpu.VMEM)
        hbm = pl.BlockSpec(memory_space=pl.ANY)
        dma = pltpu.SemaphoreType.DMA
        out = pl.pallas_call(
            functools.partial(gcn_kernel, grid_y, grid_x, chunks, big),
            out_shape=pltpu.VMEM((classes, nodes), BF16),
            in_specs=[hbm] * 6,
            out_specs=vmem,
            scratch_shapes=[
                pltpu.VMEM(send_idx.shape, jnp.int32),
                pltpu.VMEM((hidden, feat), BF16),
                pltpu.VMEM((classes, hidden), BF16),
                pltpu.VMEM((feat, nodes), BF16),
                pltpu.VMEM((nodes, nodes), BF16),
                pltpu.VMEM((nodes, nodes), BF16),
                pltpu.VMEM((nodes, slots), BF16),
                pltpu.VMEM((slots, nodes), BF16),
                pltpu.VMEM((nodes, slots), BF16),
                pltpu.VMEM((feat, half), BF16),
                pltpu.VMEM((feat, quarter), BF16),
                pltpu.VMEM((feat, quarter), BF16),
                pltpu.VMEM((feat, slots), BF16),
                pltpu.VMEM((feat, nodes), F32),
                pltpu.VMEM((512, nodes), BF16),
                pltpu.VMEM((half, slots), BF16),
                pltpu.VMEM((3 * LAST_ROWS, nodes), BF16),
                pltpu.VMEM((LAST_ROWS, slots), F32),
                pltpu.VMEM((3 * hidden, nodes), BF16),
                pltpu.VMEM((hidden, slots), F32),
                pltpu.VMEM((hidden, nodes), F32),
                pltpu.VMEM((hidden, nodes), BF16),
                pltpu.VMEM((hidden, half), BF16),
                pltpu.VMEM((hidden, quarter), BF16),
                pltpu.VMEM((hidden, quarter), BF16),
                pltpu.VMEM((hidden, half), BF16),
                pltpu.VMEM((hidden, half), BF16),
                dma((3,)),
                dma((len(chunks),)),
                dma,
                dma,
                dma((len(chunks),)),
                dma((len(chunks),)),
                dma((2 * len(big),)),
                dma((2 * len(big),)),
                dma((3,)),
                dma((3,)),
            ],
            compiler_params=pltpu.CompilerParams(collective_id=0, has_side_effects=True, vmem_limit_bytes=60 * 2**20),
        )(send_idx, w_hidden.T, w_out.T, node_feats.T, adj_int, adj_halo)
        return out.T

    return jax.shard_map(per_device, mesh=mesh, in_specs=(node_spec, node_spec, node_spec, node_spec, full_spec, full_spec), out_specs=node_spec, check_vma=False)
```

time: 42.9 us -> 41.8 us (0.974)
  Pallas kernels: 42.2 us -> 41 us
    pallas_call x1, Pallas kernels: 42.2 us -> 41 us  [per_device(): pl.pallas_call(functools.partial(gcn_kernel, grid_y, grid_x, chunks, big)...]
where the time goes in v4:
time: 41.8 us; the launch traced here: 41.6 us
  Pallas kernels  41 us (98%)
  local copies, waits for them, and re-layouts  0.62 us (1%)
    pallas_call x1, Pallas kernels, per_device(): pl.pallas_call(functools.partial(gcn_kernel, grid_y, grid_x, chunks, big)...  41 us

profile of v4, /device:TPU:0, one launch (start us, length us, event | category | flops | bytes accessed | tf_op | source)
XLA Modules:
  0.0 41.6 jit_solution(16325383567374076163)
XLA Ops:
  0.0 41.0 %shard_map.64 = bf16[7,2048]{1,0:T(8,128)(2,1)S(1)} custom-call(s32[4,256]{1,0:T(4,128)} %idx_hbm.1, bf16[16,1433]{1,0:T(8,128)(2,1)} %bitcast.6, bf16[7,16]{1,0:T(8,128)(2,1)} %bitcast.7, bf16[1433,2048]{1,0:T(8,128)(2,1)} %bitcast.5, bf16[2048,2048]{1,0:T(8,128)(2,1)} %int_hbm.1, bf16[2048,1024]{1,0:T(8,128)(2,1)} %halo_hbm.1), custom_call_target="tpu_custom_call" | custom-call | tf_op jit(solution)/shard_map/pallas_call | solution.py:252
  41.0 0.6 %copy.8 = bf16[2048,7]{0,1:T(8,128)(2,1)} copy(bf16[2048,7]{0,1:T(8,128)(2,1)S(1)} %bitcast.4) | data formatting | bytes 57344

commit v5 on v4

--- a/solution.py
+++ b/solution.py
@@ -12,7 +12,7 @@
 MESH = pl.DeviceIdType.MESH
 N_TILE = 256
 BIG_ROWS = 512
-LAST_ROWS = 96
+LAST_ROWS = 128
 BIG_COLS = 1024
 HALO_COLS = 512
 NN = (((1,), (0,)), ((), ()))
@@ -24,7 +24,7 @@
 
 
 def feature_chunks(feat):
-    last = (feat - 80) // 64 * 64
+    last = (feat - 112) // 16 * 16
     cuts = [0, 64, 256]
     while last - 128 - cuts[-1] > 256:
         cuts.append(cuts[-1] + 256)
@@ -36,7 +36,11 @@
     return [(lo, min(lo + BIG_ROWS, feat)) for lo in range(0, feat, BIG_ROWS)]
 
 
-def gcn_kernel(grid_y, grid_x, chunks, big, idx_hbm, w0_hbm, w1_hbm, feat_hbm, int_hbm, halo_hbm, out_ref,
+def x_chunks(feat):
+    return [(0, BIG_ROWS), (BIG_ROWS, feat)]
+
+
+def gcn_kernel(grid_y, grid_x, chunks, x_parts, big, idx_hbm, w0_hbm, w1_hbm, feat_hbm, int_hbm, halo_hbm, out_ref,
                idx_ref, w0_ref, w1_ref, feat_v, int_v, int_t, halo_v, halo_t, pick_v, send_y, send_x0, send_x1, recv_v, z_int, z_half, halo_pick, z_split, z_pick, hid_split, hid_pick, hid_acc,
                hid_v, send2_y, send2_x0, send2_x1, recv2_y, recv2_x,
                small_sem, feat_sem, int_sem, halo_sem, sy_sem, ry_sem, sx_sem, rx_sem, s2_sem, r2_sem):
@@ -67,14 +71,15 @@
     feat_in[0].start()
 
     def pick_block(buf, start):
-        node_ids = lax.broadcasted_iota(jnp.int32, (N_TILE, quarter), 0) + start
-        return jnp.where(node_ids == idx_ref[buf:buf + 1, :], 1.0, 0.0).astype(BF16)
-
-    def build_pick(first_buf):
+        node_ids = lax.broadcasted_iota(jnp.int16, (N_TILE, quarter), 0)
+        plan = jnp.broadcast_to(idx_ref[buf:buf + 1, :] - start, (N_TILE, quarter)).astype(jnp.int16)
+        return jnp.where(node_ids == plan, jnp.ones((), BF16), jnp.zeros((), BF16))
+
+    def build_pick(*bufs):
         @pl.loop(0, nodes // N_TILE)
         def _(blk):
             start = pl.multiple_of(blk * N_TILE, N_TILE)
-            for buf in (first_buf, first_buf + 1):
+            for buf in bufs:
                 pick_v[pl.ds(start, N_TILE), buf * quarter:(buf + 1) * quarter] = pick_block(buf, start)
 
     def remote(src, dst, send_sem, recv_sem, target):
@@ -113,7 +118,7 @@
             y_copies[-1].start()
 
     def send_x_rows(num):
-        rows = pl.ds(big[num][0], big[num][1] - big[num][0])
+        rows = pl.ds(x_parts[num][0], x_parts[num][1] - x_parts[num][0])
         with jax.named_scope(f'gather_x{num}'):
             picked = dot(feat_v[rows, :], pick_v[:, :half], NN).astype(BF16)
             send_x0[rows, :] = picked[:, :quarter]
@@ -126,13 +131,13 @@
     next_x = 0
     for first, end in [(0, 1), (1, 2), (2, 4), (4, len(chunks))]:
         send_y_rows(first, end)
+        if first == 1:
+            with jax.named_scope('pick_x'):
+                build_pick(0, 1)
         if first == 0:
             for copy in (int_in, halo_in, w0_in, w1_in):
                 copy.start()
-        if first == 1:
-            with jax.named_scope('pick_x'):
-                build_pick(0)
-        while next_x < len(big) and big[next_x][1] <= chunks[end - 1][1]:
+        while next_x < len(x_parts) and x_parts[next_x][1] <= chunks[end - 1][1]:
             send_x_rows(next_x)
             next_x += 1
 
@@ -151,9 +156,6 @@
             for lo, hi in big:
                 z_int[lo:hi, cols] = dot(feat_v[lo:hi, :], int_v[cols, :], NT)
 
-    with jax.named_scope('xwait'):
-        for copy in x_copies:
-            copy.wait_recv()
     def split3(value):
         high = value.astype(BF16)
         rest = value - high.astype(F32)
@@ -165,6 +167,9 @@
     tail = last_hi - last_lo
     with jax.named_scope('halo_pick'):
         halo_pick[...] = dot(halo_t[half:, :], pick_v[...], NN).astype(BF16)
+    with jax.named_scope('xwait'):
+        for copy in x_copies:
+            copy.wait_recv()
     with jax.named_scope('last_x'):
         z_last = z_int[last, :] + dot(recv_v[last, :half], halo_t[:half, :], NN)
         z_int[last, :] = z_last
@@ -245,12 +250,13 @@
         half, quarter = slots // 2, slots // 4
         hidden, classes = w_out.shape
         chunks = feature_chunks(feat)
+        x_parts = x_chunks(feat)
         big = big_chunks(feat)
         vmem = pl.BlockSpec(memory_space=pltpu.VMEM)
         hbm = pl.BlockSpec(memory_space=pl.ANY)
         dma = pltpu.SemaphoreType.DMA
         out = pl.pallas_call(
-            functools.partial(gcn_kernel, grid_y, grid_x, chunks, big),
+            functools.partial(gcn_kernel, grid_y, grid_x, chunks, x_parts, big),
             out_shape=pltpu.VMEM((classes, nodes), BF16),
             in_specs=[hbm] * 6,
             out_specs=vmem,
@@ -288,8 +294,8 @@
                 dma,
                 dma((len(chunks),)),
                 dma((len(chunks),)),
-                dma((2 * len(big),)),
-                dma((2 * len(big),)),
+                dma((2 * len(x_parts),)),
+                dma((2 * len(x_parts),)),
                 dma((3,)),
                 dma((3,)),
             ],

time: 41.8 us -> 41.7 us (level)
  no operation moved by 1% of the time
where the time goes in v5:
time: 41.7 us; the launch traced here: 41.6 us
  Pallas kernels  41 us (98%)
  local copies, waits for them, and re-layouts  0.62 us (1%)
    pallas_call x1, Pallas kernels, per_device(): pl.pallas_call(functools.partial(gcn_kernel, grid_y, grid_x, chunks, x_pa...  41 us

profile of v5, /device:TPU:0, one launch (start us, length us, event | category | flops | bytes accessed | tf_op | source)
XLA Modules:
  0.0 41.6 jit_solution(9144730594880729959)
XLA Ops:
  0.0 41.0 %shard_map.64 = bf16[7,2048]{1,0:T(8,128)(2,1)S(1)} custom-call(s32[4,256]{1,0:T(4,128)} %idx_hbm.1, bf16[16,1433]{1,0:T(8,128)(2,1)} %bitcast.6, bf16[7,16]{1,0:T(8,128)(2,1)} %bitcast.7, bf16[1433,2048]{1,0:T(8,128)(2,1)} %bitcast.5, bf16[2048,2048]{1,0:T(8,128)(2,1)} %int_hbm.1, bf16[2048,1024]{1,0:T(8,128)(2,1)} %halo_hbm.1), custom_call_target="tpu_custom_call" | custom-call | tf_op jit(solution)/shard_map/pallas_call | solution.py:258
  41.0 0.6 %copy.8 = bf16[2048,7]{0,1:T(8,128)(2,1)} copy(bf16[2048,7]{0,1:T(8,128)(2,1)S(1)} %bitcast.4) | data formatting | bytes 57344

commit v6 on v5

--- a/solution.py
+++ b/solution.py
@@ -12,7 +12,8 @@
 MESH = pl.DeviceIdType.MESH
 N_TILE = 256
 BIG_ROWS = 512
-LAST_ROWS = 128
+LAST_ROWS = 112
+NUM_GATHERS = 4
 BIG_COLS = 1024
 HALO_COLS = 512
 NN = (((1,), (0,)), ((), ()))
@@ -24,7 +25,7 @@
 
 
 def feature_chunks(feat):
-    last = (feat - 112) // 16 * 16
+    last = (feat - 96) // 16 * 16
     cuts = [0, 64, 256]
     while last - 128 - cuts[-1] > 256:
         cuts.append(cuts[-1] + 256)
@@ -42,26 +43,33 @@
 
 def gcn_kernel(grid_y, grid_x, chunks, x_parts, big, idx_hbm, w0_hbm, w1_hbm, feat_hbm, int_hbm, halo_hbm, out_ref,
                idx_ref, w0_ref, w1_ref, feat_v, int_v, int_t, halo_v, halo_t, pick_v, send_y, send_x0, send_x1, recv_v, z_int, z_half, halo_pick, z_split, z_pick, hid_split, hid_pick, hid_acc,
-               hid_v, send2_y, send2_x0, send2_x1, recv2_y, recv2_x,
-               small_sem, feat_sem, int_sem, halo_sem, sy_sem, ry_sem, sx_sem, rx_sem, s2_sem, r2_sem):
+               hid_v, send2_y, send2_x0, send2_x1, recv2_v,
+               small_sem, feat_sem, int_sem, halo_sem, sy_sem, ry_sem, sx_sem, rx_sem, s2_sem, r2_sem, even_sem):
     me_y = lax.axis_index('tiley')
     me_x = lax.axis_index('tilex')
     east = {'tilex': lax.rem(me_x + 1, grid_x)}
     west = {'tilex': lax.rem(me_x + grid_x - 1, grid_x)}
     north = {'tiley': lax.rem(me_y + 1, grid_y)}
     nodes = int_v.shape[0]
-    half = halo_v.shape[1] // 2
+    slots = halo_v.shape[1]
+    half = slots // 2
     quarter = half // 2
     hid_rows = hid_v.shape[0]
 
     barrier = pltpu.get_barrier_semaphore()
-    for neighbour in (north, east, west):
-        pl.semaphore_signal(barrier, inc=1, device_id=neighbour, device_id_type=MESH)
+    pl.semaphore_signal(barrier, inc=1, device_id=north, device_id_type=MESH)
+    odd = lax.rem(me_x, 2)
+
+    @pl.when(odd == 1)
+    def _():
+        for neighbour in (east, west):
+            pl.semaphore_signal(barrier, inc=1, device_id=neighbour, device_id_type=MESH)
 
     idx_in = pltpu.make_async_copy(idx_hbm, idx_ref, small_sem.at[0])
+    gathers = [(0, 1), (1, 2), (2, 4), (4, len(chunks))]
     feat_in = []
-    for num, (lo, hi) in enumerate(chunks):
-        rows = pl.ds(lo, hi - lo)
+    for num, (first, end) in enumerate(gathers):
+        rows = pl.ds(chunks[first][0], chunks[end - 1][1] - chunks[first][0])
         feat_in.append(pltpu.make_async_copy(feat_hbm.at[rows, :], feat_v.at[rows, :], feat_sem.at[num]))
     w0_in = pltpu.make_async_copy(w0_hbm, w0_ref, small_sem.at[1])
     w1_in = pltpu.make_async_copy(w1_hbm, w1_ref, small_sem.at[2])
@@ -92,29 +100,37 @@
     y_copies = []
     x_copies = []
 
-    def send_y_rows(first, end):
+    def first_piece(rows):
+        picked = None
+        for start in range(0, nodes, N_TILE):
+            block = jnp.concatenate([pick_block(2, start), pick_block(3, start)], axis=1)
+            pick_v[start:start + N_TILE, half:] = block
+            part = dot(feat_v[rows, start:start + N_TILE], block, NN)
+            picked = part if picked is None else picked + part
+        send_y[rows, :] = picked.astype(BF16)
+
+    def send_y_rows(num, first, end):
         lo, hi = chunks[first][0], chunks[end - 1][1]
         rows = pl.ds(lo, hi - lo)
         with jax.named_scope(f'feat_wait{first}'):
-            for copy in feat_in[first:end]:
-                copy.wait()
+            feat_in[num].wait()
         with jax.named_scope(f'gather_y{first}'):
-            if first == 0:
-                picked = None
-                for start in range(0, nodes, N_TILE):
-                    block = jnp.concatenate([pick_block(2, start), pick_block(3, start)], axis=1)
-                    pick_v[start:start + N_TILE, half:] = block
-                    part = dot(feat_v[rows, start:start + N_TILE], block, NN)
-                    picked = part if picked is None else picked + part
-                send_y[rows, :] = picked.astype(BF16)
+            if first > 0:
+                send_y[rows, :] = dot(feat_v[rows, :], pick_v[:, half:], NN).astype(BF16)
             else:
-                send_y[rows, :] = dot(feat_v[rows, :], pick_v[:, half:], NN).astype(BF16)
+                first_piece(rows)
         if first == 0:
             with jax.named_scope('barrier'):
-                pl.semaphore_wait(barrier, 3)
-        for num in range(first, end):
-            rows = pl.ds(chunks[num][0], chunks[num][1] - chunks[num][0])
-            y_copies.append(remote(send_y.at[rows, :], recv_v.at[rows, half:], sy_sem.at[num], ry_sem.at[num], north))
+                pl.semaphore_wait(barrier, 3 - 2 * odd)
+
+                @pl.when(odd == 0)
+                def _():
+                    for neighbour in (east, west):
+                        pl.semaphore_signal(even_sem, inc=1, device_id=neighbour, device_id_type=MESH)
+
+        for chunk in range(first, end):
+            rows = pl.ds(chunks[chunk][0], chunks[chunk][1] - chunks[chunk][0])
+            y_copies.append(remote(send_y.at[rows, :], recv_v.at[rows, half:], sy_sem, ry_sem.at[chunk], north))
             y_copies[-1].start()
 
     def send_x_rows(num):
@@ -123,14 +139,20 @@
             picked = dot(feat_v[rows, :], pick_v[:, :half], NN).astype(BF16)
             send_x0[rows, :] = picked[:, :quarter]
             send_x1[rows, :] = picked[:, quarter:]
-        x_copies.append(remote(send_x0.at[rows, :], recv_v.at[rows, :quarter], sx_sem.at[2 * num], rx_sem.at[2 * num], east))
-        x_copies.append(remote(send_x1.at[rows, :], recv_v.at[rows, quarter:half], sx_sem.at[2 * num + 1], rx_sem.at[2 * num + 1], west))
+        if num == 0:
+
+            @pl.when(odd == 1)
+            def _():
+                pl.semaphore_wait(even_sem, 2)
+
+        x_copies.append(remote(send_x0.at[rows, :], recv_v.at[rows, :quarter], sx_sem.at[0], rx_sem.at[0], east))
+        x_copies.append(remote(send_x1.at[rows, :], recv_v.at[rows, quarter:half], sx_sem.at[1], rx_sem.at[1], west))
         x_copies[-2].start()
         x_copies[-1].start()
 
     next_x = 0
-    for first, end in [(0, 1), (1, 2), (2, 4), (4, len(chunks))]:
-        send_y_rows(first, end)
+    for num, (first, end) in enumerate(gathers):
+        send_y_rows(num, first, end)
         if first == 1:
             with jax.named_scope('pick_x'):
                 build_pick(0, 1)
@@ -168,7 +190,11 @@
     with jax.named_scope('halo_pick'):
         halo_pick[...] = dot(halo_t[half:, :], pick_v[...], NN).astype(BF16)
     with jax.named_scope('xwait'):
-        for copy in x_copies:
+        x_whole = [
+            remote(send_x0, recv_v.at[:, :quarter], sx_sem.at[0], rx_sem.at[0], east),
+            remote(send_x1, recv_v.at[:, quarter:half], sx_sem.at[1], rx_sem.at[1], west),
+        ]
+        for copy in x_whole:
             copy.wait_recv()
     with jax.named_scope('last_x'):
         z_last = z_int[last, :] + dot(recv_v[last, :half], halo_t[:half, :], NN)
@@ -202,9 +228,9 @@
         hid_pick[...] = parts[:hid_rows] + parts[hid_rows:2 * hid_rows] + parts[2 * hid_rows:]
 
     second = [
-        remote(send2_y, recv2_y, s2_sem.at[0], r2_sem.at[0], north),
-        remote(send2_x0, recv2_x.at[:, :quarter], s2_sem.at[1], r2_sem.at[1], east),
-        remote(send2_x1, recv2_x.at[:, quarter:], s2_sem.at[2], r2_sem.at[2], west),
+        remote(send2_y, recv2_v.at[:, half:], s2_sem.at[0], r2_sem.at[0], north),
+        remote(send2_x0, recv2_v.at[:, :quarter], s2_sem.at[1], r2_sem.at[1], east),
+        remote(send2_x1, recv2_v.at[:, quarter:half], s2_sem.at[2], r2_sem.at[2], west),
     ]
     with jax.named_scope('ywait_last'):
         y_copies[-1].wait_recv()
@@ -223,18 +249,31 @@
         hid_v[...] = jnp.maximum(hid_sum, 0.0).astype(BF16)
     with jax.named_scope('interior2'):
         hid_acc[...] = dot(hid_v[...], int_t[...], NN)
-    with jax.named_scope('wait2x'):
-        second[1].wait_recv()
-        second[2].wait_recv()
-    with jax.named_scope('xhalo2'):
-        hid_acc[...] += dot(recv2_x[...], halo_t[:half, :], NN)
-    with jax.named_scope('wait2y'):
-        second[0].wait_recv()
-    with jax.named_scope('yhalo2'):
-        z_sum = hid_acc[...] + dot(recv2_y[...], halo_t[half:, :], NN)
+    from_y, from_west, from_east = second
+
+    def halo_part(lo, hi):
+        return dot(recv2_v[:, lo:hi], halo_t[lo:hi, :], NN)
+
+    def finish(parts):
+        z_sum = hid_acc[...]
+        for copies, lo, hi in parts:
+            for copy in copies:
+                copy.wait_recv()
+            z_sum = z_sum + halo_part(lo, hi)
         out_ref[...] = dot(w1_ref[...], z_sum.astype(BF16), NN).astype(BF16)
+
+    with jax.named_scope('halo2'):
+
+        @pl.when(odd == 1)
+        def _():
+            finish([([from_y], half, slots), ([from_west, from_east], 0, half)])
+
+        @pl.when(odd == 0)
+        def _():
+            finish([([from_west, from_east], 0, half), ([from_y], half, slots)])
+
     with jax.named_scope('sendwait'):
-        for copy in y_copies + x_copies + second:
+        for copy in [remote(send_y, recv_v.at[:, half:], sy_sem, ry_sem.at[0], north)] + x_whole + second:
             copy.wait_send()
 
 
@@ -286,18 +325,18 @@
                 pltpu.VMEM((hidden, half), BF16),
                 pltpu.VMEM((hidden, quarter), BF16),
                 pltpu.VMEM((hidden, quarter), BF16),
-                pltpu.VMEM((hidden, half), BF16),
-                pltpu.VMEM((hidden, half), BF16),
+                pltpu.VMEM((hidden, slots), BF16),
                 dma((3,)),
-                dma((len(chunks),)),
+                dma((NUM_GATHERS,)),
+                dma,
                 dma,
                 dma,
                 dma((len(chunks),)),
-                dma((len(chunks),)),
-                dma((2 * len(x_parts),)),
-                dma((2 * len(x_parts),)),
+                dma((2,)),
+                dma((2,)),
                 dma((3,)),
                 dma((3,)),
+                pltpu.SemaphoreType.REGULAR,
             ],
             compiler_params=pltpu.CompilerParams(collective_id=0, has_side_effects=True, vmem_limit_bytes=60 * 2**20),
         )(send_idx, w_hidden.T, w_out.T, node_feats.T, adj_int, adj_halo)

time: 41.7 us -> 41.4 us (level)
  no operation moved by 1% of the time
where the time goes in v6:
time: 41.4 us; the launch traced here: 41.3 us
  Pallas kernels  40.7 us (98%)
  local copies, waits for them, and re-layouts  0.62 us (1%)
    pallas_call x1, Pallas kernels, per_device(): pl.pallas_call(functools.partial(gcn_kernel, grid_y, grid_x, chunks, x_pa...  40.7 us

profile of v6, /device:TPU:0, one launch (start us, length us, event | category | flops | bytes accessed | tf_op | source)
XLA Modules:
  0.0 41.3 jit_solution(1942247214955795180)
XLA Ops:
  0.0 40.7 %shard_map.64 = bf16[7,2048]{1,0:T(8,128)(2,1)S(1)} custom-call(s32[4,256]{1,0:T(4,128)} %idx_hbm.1, bf16[16,1433]{1,0:T(8,128)(2,1)} %bitcast.6, bf16[7,16]{1,0:T(8,128)(2,1)} %bitcast.7, bf16[1433,2048]{1,0:T(8,128)(2,1)} %bitcast.5, bf16[2048,2048]{1,0:T(8,128)(2,1)} %int_hbm.1, bf16[2048,1024]{1,0:T(8,128)(2,1)} %halo_hbm.1), custom_call_target="tpu_custom_call" | custom-call | tf_op jit(solution)/shard_map/pallas_call | solution.py:297
  40.7 0.6 %copy.8 = bf16[2048,7]{0,1:T(8,128)(2,1)} copy(bf16[2048,7]{0,1:T(8,128)(2,1)S(1)} %bitcast.4) | data formatting | bytes 57344

commit v7 on v6

--- a/solution.py
+++ b/solution.py
@@ -14,7 +14,7 @@
 BIG_ROWS = 512
 LAST_ROWS = 112
 NUM_GATHERS = 4
-BIG_COLS = 1024
+BIG_COLS = 2048
 HALO_COLS = 512
 NN = (((1,), (0,)), ((), ()))
 NT = (((1,), (1,)), ((), ()))
@@ -256,9 +256,10 @@
 
     def finish(parts):
         z_sum = hid_acc[...]
-        for copies, lo, hi in parts:
-            for copy in copies:
-                copy.wait_recv()
+        for num, (copies, lo, hi) in enumerate(parts):
+            with jax.named_scope(f'finwait{num}'):
+                for copy in copies:
+                    copy.wait_recv()
             z_sum = z_sum + halo_part(lo, hi)
         out_ref[...] = dot(w1_ref[...], z_sum.astype(BF16), NN).astype(BF16)
 
@@ -266,11 +267,11 @@
 
         @pl.when(odd == 1)
         def _():
-            finish([([from_y], half, slots), ([from_west, from_east], 0, half)])
+            finish([([from_y], half, slots), ([from_west], 0, quarter), ([from_east], quarter, half)])
 
         @pl.when(odd == 0)
         def _():
-            finish([([from_west, from_east], 0, half), ([from_y], half, slots)])
+            finish([([from_east], quarter, half), ([from_west], 0, quarter), ([from_y], half, slots)])
 
     with jax.named_scope('sendwait'):
         for copy in [remote(send_y, recv_v.at[:, half:], sy_sem, ry_sem.at[0], north)] + x_whole + second:

time: 41.4 us -> 41.3 us (level)
  no operation moved by 1% of the time
where the time goes in v7:
time: 41.3 us; the launch traced here: 41.2 us
  Pallas kernels  40.6 us (98%)
  local copies, waits for them, and re-layouts  0.62 us (2%)
    pallas_call x1, Pallas kernels, per_device(): pl.pallas_call(functools.partial(gcn_kernel, grid_y, grid_x, chunks, x_pa...  40.6 us

profile of v7, /device:TPU:0, one launch (start us, length us, event | category | flops | bytes accessed | tf_op | source)
XLA Modules:
  0.0 41.2 jit_solution(12372392517235290556)
XLA Ops:
  0.0 40.6 %shard_map.64 = bf16[7,2048]{1,0:T(8,128)(2,1)S(1)} custom-call(s32[4,256]{1,0:T(4,128)} %idx_hbm.1, bf16[16,1433]{1,0:T(8,128)(2,1)} %bitcast.6, bf16[7,16]{1,0:T(8,128)(2,1)} %bitcast.7, bf16[1433,2048]{1,0:T(8,128)(2,1)} %bitcast.5, bf16[2048,2048]{1,0:T(8,128)(2,1)} %int_hbm.1, bf16[2048,1024]{1,0:T(8,128)(2,1)} %halo_hbm.1), custom_call_target="tpu_custom_call" | custom-call | tf_op jit(solution)/shard_map/pallas_call | solution.py:298
  40.6 0.6 %copy.8 = bf16[2048,7]{0,1:T(8,128)(2,1)} copy(bf16[2048,7]{0,1:T(8,128)(2,1)S(1)} %bitcast.4) | data formatting | bytes 57344

commit v8 on v7

--- a/solution.py
+++ b/solution.py
@@ -42,8 +42,8 @@
 
 
 def gcn_kernel(grid_y, grid_x, chunks, x_parts, big, idx_hbm, w0_hbm, w1_hbm, feat_hbm, int_hbm, halo_hbm, out_ref,
-               idx_ref, w0_ref, w1_ref, feat_v, int_v, int_t, halo_v, halo_t, pick_v, send_y, send_x0, send_x1, recv_v, z_int, z_half, halo_pick, z_split, z_pick, hid_split, hid_pick, hid_acc,
-               hid_v, send2_y, send2_x0, send2_x1, recv2_v,
+               idx_ref, w0_ref, w1_ref, feat_v, int_v, int_t, halo_v, halo_t, pick_v, send_y, send_x, recv_v, z_int, z_half, halo_pick, z_split, z_pick, hid_split, hid_pick, hid_acc,
+               hid_v, send2_v, recv2_v,
                small_sem, feat_sem, int_sem, halo_sem, sy_sem, ry_sem, sx_sem, rx_sem, s2_sem, r2_sem, even_sem):
     me_y = lax.axis_index('tiley')
     me_x = lax.axis_index('tilex')
@@ -130,23 +130,22 @@
 
         for chunk in range(first, end):
             rows = pl.ds(chunks[chunk][0], chunks[chunk][1] - chunks[chunk][0])
-            y_copies.append(remote(send_y.at[rows, :], recv_v.at[rows, half:], sy_sem, ry_sem.at[chunk], north))
+            y_copies.append(remote(send_y.at[rows, :], recv_v.at[rows, half:], sy_sem, ry_sem.at[max(chunk - 2, 0)], north))
             y_copies[-1].start()
 
     def send_x_rows(num):
         rows = pl.ds(x_parts[num][0], x_parts[num][1] - x_parts[num][0])
         with jax.named_scope(f'gather_x{num}'):
             picked = dot(feat_v[rows, :], pick_v[:, :half], NN).astype(BF16)
-            send_x0[rows, :] = picked[:, :quarter]
-            send_x1[rows, :] = picked[:, quarter:]
+            send_x[rows, :] = picked
         if num == 0:
 
             @pl.when(odd == 1)
             def _():
                 pl.semaphore_wait(even_sem, 2)
 
-        x_copies.append(remote(send_x0.at[rows, :], recv_v.at[rows, :quarter], sx_sem.at[0], rx_sem.at[0], east))
-        x_copies.append(remote(send_x1.at[rows, :], recv_v.at[rows, quarter:half], sx_sem.at[1], rx_sem.at[1], west))
+        x_copies.append(remote(send_x.at[rows, :quarter], recv_v.at[rows, :quarter], sx_sem, rx_sem, east))
+        x_copies.append(remote(send_x.at[rows, quarter:], recv_v.at[rows, quarter:half], sx_sem, rx_sem, west))
         x_copies[-2].start()
         x_copies[-1].start()
 
@@ -190,12 +189,8 @@
     with jax.named_scope('halo_pick'):
         halo_pick[...] = dot(halo_t[half:, :], pick_v[...], NN).astype(BF16)
     with jax.named_scope('xwait'):
-        x_whole = [
-            remote(send_x0, recv_v.at[:, :quarter], sx_sem.at[0], rx_sem.at[0], east),
-            remote(send_x1, recv_v.at[:, quarter:half], sx_sem.at[1], rx_sem.at[1], west),
-        ]
-        for copy in x_whole:
-            copy.wait_recv()
+        x_whole = remote(send_x, recv_v.at[:, :half], sx_sem, rx_sem, east)
+        x_whole.wait_recv()
     with jax.named_scope('last_x'):
         z_last = z_int[last, :] + dot(recv_v[last, :half], halo_t[:half, :], NN)
         z_int[last, :] = z_last
@@ -209,9 +204,8 @@
     for first, end in groups:
         lo, hi = chunks[first][0], chunks[end - 1][1]
         with jax.named_scope(f'ywait{first}'):
-            for copy in y_copies[first:end]:
-                copy.wait_recv()
-        rows = pl.ds(lo, hi - lo)
+            rows = pl.ds(lo, hi - lo)
+            remote(send_y.at[rows, :], recv_v.at[rows, half:], sy_sem, ry_sem.at[max(first - 2, 0)], north).wait_recv()
         with jax.named_scope(f'yhalo{first}'):
             for col in range(0, nodes, HALO_COLS):
                 cols = pl.ds(col, HALO_COLS)
@@ -228,19 +222,16 @@
         hid_pick[...] = parts[:hid_rows] + parts[hid_rows:2 * hid_rows] + parts[2 * hid_rows:]
 
     second = [
-        remote(send2_y, recv2_v.at[:, half:], s2_sem.at[0], r2_sem.at[0], north),
-        remote(send2_x0, recv2_v.at[:, :quarter], s2_sem.at[1], r2_sem.at[1], east),
-        remote(send2_x1, recv2_v.at[:, quarter:half], s2_sem.at[2], r2_sem.at[2], west),
+        remote(send2_v.at[:, half:], recv2_v.at[:, half:], s2_sem, r2_sem.at[0], north),
+        remote(send2_v.at[:, :quarter], recv2_v.at[:, :quarter], s2_sem, r2_sem.at[1], east),
+        remote(send2_v.at[:, quarter:half], recv2_v.at[:, quarter:half], s2_sem, r2_sem.at[2], west),
     ]
     with jax.named_scope('ywait_last'):
         y_copies[-1].wait_recv()
     with jax.named_scope('sent2'):
         z_sent = (z_pick[:tail, :] + dot(recv_v[last, half:], halo_pick[...], NN)).astype(BF16)
         sent = hid_pick[...] + dot(w0_ref[:, last_lo:last_hi], z_sent, NN)
-        sent = jnp.maximum(sent, 0.0).astype(BF16)
-        send2_y[...] = sent[:, half:]
-        send2_x0[...] = sent[:, :quarter]
-        send2_x1[...] = sent[:, quarter:half]
+        send2_v[...] = jnp.maximum(sent, 0.0).astype(BF16)
     for copy in second:
         copy.start()
     with jax.named_scope('yhalo_last'):
@@ -274,7 +265,11 @@
             finish([([from_east], quarter, half), ([from_west], 0, quarter), ([from_y], half, slots)])
 
     with jax.named_scope('sendwait'):
-        for copy in [remote(send_y, recv_v.at[:, half:], sy_sem, ry_sem.at[0], north)] + x_whole + second:
+        for copy in (
+            remote(send_y, recv_v.at[:, half:], sy_sem, ry_sem.at[0], north),
+            x_whole,
+            remote(send2_v, recv2_v, s2_sem, r2_sem.at[0], north),
+        ):
             copy.wait_send()
 
 
@@ -311,8 +306,7 @@
                 pltpu.VMEM((slots, nodes), BF16),
                 pltpu.VMEM((nodes, slots), BF16),
                 pltpu.VMEM((feat, half), BF16),
-                pltpu.VMEM((feat, quarter), BF16),
-                pltpu.VMEM((feat, quarter), BF16),
+                pltpu.VMEM((feat, half), BF16),
                 pltpu.VMEM((feat, slots), BF16),
                 pltpu.VMEM((feat, nodes), F32),
                 pltpu.VMEM((512, nodes), BF16),
@@ -323,19 +317,17 @@
                 pltpu.VMEM((hidden, slots), F32),
                 pltpu.VMEM((hidden, nodes), F32),
                 pltpu.VMEM((hidden, nodes), BF16),
-                pltpu.VMEM((hidden, half), BF16),
-                pltpu.VMEM((hidden, quarter), BF16),
-                pltpu.VMEM((hidden, quarter), BF16),
+                pltpu.VMEM((hidden, slots), BF16),
                 pltpu.VMEM((hidden, slots), BF16),
                 dma((3,)),
                 dma((NUM_GATHERS,)),
                 dma,
                 dma,
                 dma,
-                dma((len(chunks),)),
-                dma((2,)),
-                dma((2,)),
-                dma((3,)),
+                dma((len(chunks) - 2,)),
+                dma,
+                dma,
+                dma,
                 dma((3,)),
                 pltpu.SemaphoreType.REGULAR,
             ],

time: 41.3 us -> 41.2 us (level)
  no operation moved by 1% of the time
where the time goes in v8:
time: 41.2 us; the launch traced here: 41.1 us
  Pallas kernels  40.5 us (98%)
  local copies, waits for them, and re-layouts  0.62 us (2%)
    pallas_call x1, Pallas kernels, per_device(): pl.pallas_call(functools.partial(gcn_kernel, grid_y, grid_x, chunks, x_pa...  40.5 us

profile of v8, /device:TPU:0, one launch (start us, length us, event | category | flops | bytes accessed | tf_op | source)
XLA Modules:
  0.0 41.1 jit_solution(2546929423451775219)
XLA Ops:
  0.0 40.5 %shard_map.64 = bf16[7,2048]{1,0:T(8,128)(2,1)S(1)} custom-call(s32[4,256]{1,0:T(4,128)} %idx_hbm.1, bf16[16,1433]{1,0:T(8,128)(2,1)} %bitcast.6, bf16[7,16]{1,0:T(8,128)(2,1)} %bitcast.7, bf16[1433,2048]{1,0:T(8,128)(2,1)} %bitcast.5, bf16[2048,2048]{1,0:T(8,128)(2,1)} %int_hbm.1, bf16[2048,1024]{1,0:T(8,128)(2,1)} %halo_hbm.1), custom_call_target="tpu_custom_call" | custom-call | tf_op jit(solution)/shard_map/pallas_call | solution.py:293
  40.5 0.6 %copy.8 = bf16[2048,7]{0,1:T(8,128)(2,1)} copy(bf16[2048,7]{0,1:T(8,128)(2,1)S(1)} %bitcast.4) | data formatting | bytes 57344

commit v9 on v8

--- a/solution.py
+++ b/solution.py
@@ -13,7 +13,7 @@
 N_TILE = 256
 BIG_ROWS = 512
 LAST_ROWS = 112
-NUM_GATHERS = 4
+NUM_GATHERS = 3
 BIG_COLS = 2048
 HALO_COLS = 512
 NN = (((1,), (0,)), ((), ()))
@@ -68,7 +68,7 @@
     idx_in = pltpu.make_async_copy(idx_hbm, idx_ref, small_sem.at[0])
     gathers = [(0, 1), (1, 2), (2, 4), (4, len(chunks))]
     feat_in = []
-    for num, (first, end) in enumerate(gathers):
+    for num, (first, end) in enumerate(gathers[:2] + [(2, len(chunks))]):
         rows = pl.ds(chunks[first][0], chunks[end - 1][1] - chunks[first][0])
         feat_in.append(pltpu.make_async_copy(feat_hbm.at[rows, :], feat_v.at[rows, :], feat_sem.at[num]))
     w0_in = pltpu.make_async_copy(w0_hbm, w0_ref, small_sem.at[1])
@@ -113,7 +113,8 @@
         lo, hi = chunks[first][0], chunks[end - 1][1]
         rows = pl.ds(lo, hi - lo)
         with jax.named_scope(f'feat_wait{first}'):
-            feat_in[num].wait()
+            if num < len(feat_in):
+                feat_in[num].wait()
         with jax.named_scope(f'gather_y{first}'):
             if first > 0:
                 send_y[rows, :] = dot(feat_v[rows, :], pick_v[:, half:], NN).astype(BF16)

time: 41.2 us -> 41.2 us (level)
  no operation moved by 1% of the time
where the time goes in v9:
time: 41.2 us; the launch traced here: 41.1 us
  Pallas kernels  40.5 us (98%)
  local copies, waits for them, and re-layouts  0.62 us (2%)
    pallas_call x1, Pallas kernels, per_device(): pl.pallas_call(functools.partial(gcn_kernel, grid_y, grid_x, chunks, x_pa...  40.5 us

profile of v9, /device:TPU:0, one launch (start us, length us, event | category | flops | bytes accessed | tf_op | source)
XLA Modules:
  0.0 41.1 jit_solution(13630604604608909558)
XLA Ops:
  0.0 40.5 %shard_map.64 = bf16[7,2048]{1,0:T(8,128)(2,1)S(1)} custom-call(s32[4,256]{1,0:T(4,128)} %idx_hbm.1, bf16[16,1433]{1,0:T(8,128)(2,1)} %bitcast.6, bf16[7,16]{1,0:T(8,128)(2,1)} %bitcast.7, bf16[1433,2048]{1,0:T(8,128)(2,1)} %bitcast.5, bf16[2048,2048]{1,0:T(8,128)(2,1)} %int_hbm.1, bf16[2048,1024]{1,0:T(8,128)(2,1)} %halo_hbm.1), custom_call_target="tpu_custom_call" | custom-call | tf_op jit(solution)/shard_map/pallas_call | solution.py:294
  40.5 0.6 %copy.8 = bf16[2048,7]{0,1:T(8,128)(2,1)} copy(bf16[2048,7]{0,1:T(8,128)(2,1)S(1)} %bitcast.4) | data formatting | bytes 57344
